TPU v7x, 32 devices: a whole 2x2x4 slice. The times are simulated.
32 devices in a mesh: samp: 16 (over z, y, core), snp: 2 (over x).
Axes of the slice: x: 2, y: 2, z: 4, core: 2. Of those that a mesh axis runs over, the one named last changes fastest.
Arguments:
- genotypes: float32 [8192, 2048], P('samp', 'snp'), may hold values from 0 to 2, as said below
- observed: int32 [8192, 2048], P('samp', 'snp'), may hold values from 0 to 1
Outputs:
- relation: float32 [16, 2, 256, 8192], P(None, 'snp', None, 'samp')
Inputs may be any that keep to these rules, and one draw needn't show every extreme that they name: `genotypes`: dosages are real numbers between 0 and 2.
All inputs are finite; a program needn't handle non-finite values.
Results may differ from a plain program's by a relative error of at most 0.00061.
Values may be sent and summed in bfloat16 or wider, within the bound.
A program may use at most 128 MiB of HBM per device.

v0:
```python
import functools

import jax
import jax.numpy as jnp
from jax import lax
from jax.experimental import pallas as pl
from jax.experimental.pallas import tpu as pltpu
from jax.sharding import PartitionSpec as P

MESH = pl.DeviceIdType.MESH
var_floor = 0.1
UP, DOWN, SIDE, CORE = 0, 1, 2, 3
STRIP = 64
PIECES = 2
LOADS = 4
VMEM_ALL = 67043328
VMEM_SPARE = 512 * 1024
VMEM_FINISH = 12 * 1024 * 1024


def index(at_z, at_y, at_core):
    return at_z * 4 + at_y * 2 + at_core


def source_at(z, depth, i):
    pairs = jnp.minimum(z, depth - 1 - z)
    side = jnp.where(i % 2 == 1, z - (i + 1) // 2, z + i // 2)
    far = jnp.where(z < depth - 1 - z, z + i - pairs, z - i + pairs)
    return jnp.where(i <= 2 * pairs, side, far)


def turned_at(z, depth):
    return jnp.where(z < depth - 1, z + 1, depth - 2)


def product(rows, panel, q, parts):
    pieces, piece_rows, snp_count = rows.shape[2:]
    total = None
    for h in parts:
        block = rows[q, h].reshape(pieces * piece_rows, snp_count)
        term = lax.dot_general(block, panel[h], (((1,), (1,)), ((), ())), preferred_element_type=jnp.float32)
        total = term if total is None else total + term
    return total * (1.0 / (rows.shape[1] * snp_count))


def finish(shards, groups, rows, panel, tiles, out_ref, late, out_sem):
    depth = shards // 4
    me = lax.axis_index("samp")
    z, y = me // 4, (me // 2) % 2
    turned = turned_at(z, depth)
    final = source_at(z, depth, depth - 1)
    final = jnp.where(final == turned, source_at(z, depth, depth - 2), final)
    last_part = lax.rem(lax.axis_index("snp") + groups - 1, groups)

    def is_late(q):
        return ((q // 4 == turned) | (q // 4 == final)) & ((q // 2) % 2 != y)

    def put(q, carry):
        @pl.when(jnp.logical_not(is_late(q)))
        def _():
            pltpu.make_async_copy(tiles.at[q], out_ref.at[q, 0], out_sem.at[q]).start()

        return carry

    lax.fori_loop(0, shards, put, 0)

    def form(i, carry):
        q = index(jnp.where(i // 2 == 0, final, turned), 1 - y, lax.rem(i, 2))
        late[i] = tiles[q] + product(rows, panel, q, [last_part])
        pltpu.make_async_copy(late.at[i], out_ref.at[q, 0], out_sem.at[q]).start()
        return carry

    lax.fori_loop(0, 4, form, 0)

    def flush(q, carry):
        pltpu.make_async_copy(tiles.at[q], out_ref.at[q, 0], out_sem.at[q]).wait()
        return carry

    lax.fori_loop(0, shards, flush, 0)


def kernel(shards, groups, geno_hbm, obs_hbm, panel, rows, tiles, geno_ref, obs_ref, counts, load_sem,
           count_send, count_recv, panel_send, panel_recv, row_send, row_recv):
    row_count, snp_count = geno_ref.shape
    tile_rows = row_count // groups
    piece_rows = tile_rows // PIECES
    depth = shards // 4
    me = lax.axis_index("samp")
    part = lax.axis_index("snp")
    z, y, core = me // 4, (me // 2) % 2, me % 2

    load_rows = row_count // LOADS

    def load(i):
        block = pl.ds(pl.multiple_of(i * load_rows, load_rows), load_rows)
        return (pltpu.make_async_copy(geno_hbm.at[block], geno_ref.at[block], load_sem.at[0, i]),
                pltpu.make_async_copy(obs_hbm.at[block], obs_ref.at[block], load_sem.at[1, i]))

    for i in range(LOADS):
        for copy in load(i):
            copy.start()

    barrier = pltpu.get_barrier_semaphore()
    for step in range(1, shards):
        pl.semaphore_signal(barrier, inc=1, device_id={"samp": lax.rem(me + step, shards)}, device_id_type=MESH)
    for step in range(1, groups):
        pl.semaphore_signal(barrier, inc=1, device_id={"snp": lax.rem(part + step, groups)}, device_id_type=MESH)

    def add_strip(i, total):
        alt, call = total
        strip = pl.ds(pl.multiple_of(i * STRIP, STRIP), STRIP)
        present = obs_ref[strip, :].astype(jnp.float32)
        held = present * geno_ref[strip, :]
        for r in range(0, STRIP, 8):
            alt = alt + held[r:r + 8]
            call = call + present[r:r + 8]
        return alt, call

    zero = jnp.zeros((8, snp_count), jnp.float32)
    alt, call = zero, zero
    strips = load_rows // STRIP
    for i in range(LOADS):
        for copy in load(i):
            copy.wait()
        alt, call = lax.fori_loop(i * strips, (i + 1) * strips, add_strip, (alt, call))
    counts[me, 0:1, :] = jnp.sum(alt, axis=0, keepdims=True)
    counts[me, 1:2, :] = jnp.sum(call, axis=0, keepdims=True)

    pl.semaphore_wait(barrier, shards + groups - 2)

    def count_copy(owner, to):
        return pltpu.make_async_remote_copy(
            src_ref=counts.at[owner], dst_ref=counts.at[owner], send_sem=count_send.at[to],
            recv_sem=count_recv.at[owner], device_id={"samp": to}, device_id_type=MESH)

    for step in range(1, shards):
        count_copy(me, lax.rem(me + step, shards)).start()
    for step in range(1, shards):
        other = lax.rem(me + step, shards)
        count_copy(other, other).wait_recv()
    sums = counts[0]
    for s in range(1, shards):
        sums = sums + counts[s]
    frequency = sums[0:1] / (2.0 * jnp.maximum(sums[1:2], 1.0))
    shift = 2.0 * frequency
    gain = lax.rsqrt(jnp.maximum(shift * (1.0 - frequency), var_floor))

    def piece_of(k, p):
        return pl.ds(pl.multiple_of(k * tile_rows + p * piece_rows, piece_rows), piece_rows)

    def panel_copy(h, k, to, p):
        block = panel.at[h, piece_of(k, p)]
        return pltpu.make_async_remote_copy(
            src_ref=block, dst_ref=block, send_sem=panel_send.at[to, k, p],
            recv_sem=panel_recv.at[h, k, p], device_id={"snp": to}, device_id_type=MESH)

    strip_rows = min(STRIP, piece_rows)

    def scale_piece(k, p):
        def scale_strip(i, carry):
            start = pl.multiple_of(k * tile_rows + p * piece_rows + i * strip_rows, strip_rows)
            strip = pl.ds(start, strip_rows)
            present = obs_ref[strip, :].astype(jnp.float32)
            panel[part, strip, :] = (present * (geno_ref[strip, :] - shift) * gain).astype(jnp.bfloat16)
            return carry

        lax.fori_loop(0, piece_rows // strip_rows, scale_strip, 0)

    def row_copy(q, h, p, way, src=None):
        to = (index(z + 1, y, core), index(z - 1, y, core), index(z, 1 - y, core), index(z, y, 1 - core))[way]
        return pltpu.make_async_remote_copy(
            src_ref=rows.at[q, h, p] if src is None else src, dst_ref=rows.at[q, h, p],
            send_sem=row_send.at[way, q, h, p], recv_sem=row_recv.at[q, h, p],
            device_id={"samp": to}, device_id_type=MESH)

    def arrive(q, h, p):
        row_copy(q, h, p, CORE).wait_recv()

    last_part = lax.rem(part + groups - 1, groups)
    turned = turned_at(z, depth)

    def part_at(i):
        return lax.rem(part + i, groups)

    def send_own(h, p):
        mine = panel.at[h, piece_of(part, p)]
        row_copy(me, h, p, SIDE, mine).start()

        @pl.when(z < depth - 1)
        def _():
            row_copy(me, h, p, UP, mine).start()

        @pl.when(z > 0)
        def _():
            row_copy(me, h, p, DOWN, mine).start()

        row_copy(me, h, p, CORE, mine).start()
        rows[me, h, p] = panel[h, piece_of(part, p), :]

    for p in range(PIECES):
        for step in range(1, groups):
            other = part_at(step)
            scale_piece(other, p)
            panel_copy(part, other, other, p).start()
        scale_piece(part, p)
        send_own(part, p)
    for step in range(1, groups):
        other = part_at(step)
        for k in range(1, groups):
            for p in range(PIECES):
                panel_copy(part, lax.rem(other + k, groups), other, p).start()
    for step in range(1, groups):
        h = part_at(step)
        for p in range(PIECES):
            panel_copy(h, part, h, p).wait_recv()
            send_own(h, p)

    def column_arrival(at_z, h, p, way):
        q = index(at_z, y, core)
        arrive(q, h, p)

        @pl.when(z < depth - 1 if way == UP else z > 0)
        def _():
            row_copy(q, h, p, way).start()

        @pl.when((at_z != turned) | (h != last_part))
        def _():
            row_copy(q, h, p, SIDE).start()

        row_copy(q, h, p, CORE).start()

    def column_arrivals(i):
        def per_piece(t, carry):
            h, p = part_at(t // PIECES), lax.rem(t, PIECES)

            @pl.when(z - i >= 0)
            def _():
                column_arrival(z - i, h, p, UP)

            @pl.when(z + i < depth)
            def _():
                column_arrival(z + i, h, p, DOWN)

            return carry

        lax.fori_loop(0, groups * PIECES, per_piece, 0)

    def arrive_all(q):
        def per_piece(t, carry):
            arrive(q, t // PIECES, lax.rem(t, PIECES))
            return carry

        lax.fori_loop(0, groups * PIECES, per_piece, 0)

    def products(at_z, at_y):
        def per_core(t, carry):
            q = index(at_z, at_y, lax.rem(core + t, 2))

            @pl.when(t == 1)
            def _():
                arrive_all(q)

            tiles[q] = product(rows, panel, q, range(groups))
            return carry

        lax.fori_loop(0, 2, per_core, 0)

    def side_arrival(at_z, h, p):
        q = index(at_z, 1 - y, core)
        arrive(q, h, p)
        row_copy(q, h, p, CORE).start()

    final = source_at(z, depth, depth - 1)
    final = jnp.where(final == turned, source_at(z, depth, depth - 2), final)

    def begin_late():
        def per_tile(t, carry):
            q = index(jnp.where(t % 2 == 0, turned, final), 1 - y, lax.rem(core + t // 2, 2))

            @pl.when(t >= 2)
            def _():
                for step in range(groups - 1):
                    for p in range(PIECES):
                        arrive(q, part_at(step), p)

            tiles[q] = product(rows, panel, q, [part_at(step) for step in range(groups - 1)])
            return carry

        lax.fori_loop(0, 4, per_tile, 0)

    def round_of(i, carry):
        @pl.when(i < depth)
        def _():
            column_arrivals(i)

        @pl.when(i == 1)
        def _():
            for step in range(1, groups):
                h = part_at(step)
                for k in range(1, groups):
                    for p in range(PIECES):
                        panel_copy(h, part_at(k), h, p).wait_recv()

        @pl.when(i == depth - 1)
        def _():
            q = index(z, 1 - y, core)

            @pl.when(z > 0)
            def _():
                for p in range(PIECES):
                    row_copy(q, last_part, p, DOWN).start()

            @pl.when(z == depth - 2)
            def _():
                for p in range(PIECES):
                    row_copy(q, last_part, p, UP).start()

        at_z = source_at(z, depth, i - 1)
        products(at_z, y)

        def per_piece(t, c):
            @pl.when((i == depth) & (t == (groups - 1) * PIECES))
            def _():
                begin_late()

            @pl.when((at_z != turned) | (t // PIECES != groups - 1))
            def _():
                side_arrival(at_z, part_at(t // PIECES), lax.rem(t, PIECES))

            return c

        lax.fori_loop(0, groups * PIECES, per_piece, 0)

        @pl.when((at_z != turned) & (at_z != final))
        def _():
            products(at_z, 1 - y)

        return carry

    lax.fori_loop(1, depth + 1, round_of, 0)
    for p in range(PIECES):
        side_arrival(turned, last_part, p)
    for p in range(PIECES):
        arrive(index(final, 1 - y, 1 - core), last_part, p)
        arrive(index(turned, 1 - y, 1 - core), last_part, p)

    for step in range(1, shards):
        count_copy(me, lax.rem(me + step, shards)).wait_send()
    for step in range(1, groups):
        for k in range(groups):
            for p in range(PIECES):
                panel_copy(part, k, part_at(step), p).wait_send()

    def drain(i, carry):
        at_z, h, p = i // (groups * PIECES), lax.rem(i // PIECES, groups), lax.rem(i, PIECES)
        q = index(at_z, y, core)
        across = index(at_z, 1 - y, core)

        @pl.when((at_z <= z) & (z < depth - 1))
        def _():
            row_copy(q, h, p, UP).wait_send()

        @pl.when((at_z >= z) & (z > 0))
        def _():
            row_copy(q, h, p, DOWN).wait_send()

        @pl.when((at_z != turned) | (h != last_part))
        def _():
            row_copy(q, h, p, SIDE).wait_send()

        row_copy(q, h, p, CORE).wait_send()
        row_copy(across, h, p, CORE).wait_send()

        @pl.when((at_z == z) & (h == last_part) & (z > 0))
        def _():
            row_copy(across, h, p, DOWN).wait_send()

        @pl.when((at_z == z) & (h == last_part) & (z == depth - 2))
        def _():
            row_copy(across, h, p, UP).wait_send()

        return carry

    lax.fori_loop(0, depth * groups * PIECES, drain, 0)


def solution(mesh):
    shards, groups = mesh.shape["samp"], mesh.shape["snp"]

    def body(genotypes, observed):
        row_count, snp_count = genotypes.shape
        tile_rows = row_count // groups
        piece_rows = tile_rows // PIECES
        kept = 2 * (groups * row_count * snp_count) * (1 + shards // groups) + 4 * shards * tile_rows * row_count
        panel, rows, tiles = pl.pallas_call(
            functools.partial(kernel, shards, groups),
            out_shape=(
                pltpu.VMEM((groups, row_count, snp_count), jnp.bfloat16),
                pltpu.VMEM((shards, groups, PIECES, piece_rows, snp_count), jnp.bfloat16),
                pltpu.VMEM((shards, tile_rows, row_count), jnp.float32),
            ),
            in_specs=[pl.BlockSpec(memory_space=pltpu.HBM)] * 2,
            out_specs=[pl.BlockSpec(memory_space=pltpu.VMEM)] * 3,
            scratch_shapes=[
                pltpu.VMEM((row_count, snp_count), jnp.float32),
                pltpu.VMEM((row_count, snp_count), jnp.int32),
                pltpu.VMEM((shards, 2, snp_count), jnp.float32),
                pltpu.SemaphoreType.DMA((2, LOADS)),
                pltpu.SemaphoreType.DMA((shards,)),
                pltpu.SemaphoreType.DMA((shards,)),
                pltpu.SemaphoreType.DMA((groups, groups, PIECES)),
                pltpu.SemaphoreType.DMA((groups, groups, PIECES)),
                pltpu.SemaphoreType.DMA((4, shards, groups, PIECES)),
                pltpu.SemaphoreType.DMA((shards, groups, PIECES)),
            ],
            compiler_params=pltpu.CompilerParams(
                collective_id=0, has_side_effects=True, vmem_limit_bytes=VMEM_ALL - VMEM_SPARE - kept),
        )(genotypes, observed)
        return pl.pallas_call(
            functools.partial(finish, shards, groups),
            out_shape=jax.ShapeDtypeStruct((shards, 1, tile_rows, row_count), jnp.float32),
            in_specs=[pl.BlockSpec(memory_space=pltpu.VMEM)] * 3,
            out_specs=pl.BlockSpec(memory_space=pltpu.HBM),
            scratch_shapes=[
                pltpu.VMEM((4, tile_rows, row_count), jnp.float32),
                pltpu.SemaphoreType.DMA((shards,)),
            ],
            compiler_params=pltpu.CompilerParams(vmem_limit_bytes=VMEM_FINISH),
        )(rows, panel, tiles)

    return jax.shard_map(
        body,
        mesh=mesh,
        in_specs=(P("samp", "snp"), P("samp", "snp")),
        out_specs=P(None, "snp", None, "samp"),
        check_vma=False,
    )
```

profile of v0, /device:TPU:0, one launch (start us, length us, event | category | flops | bytes accessed | tf_op | source)
XLA Modules:
  0.0 100.3 jit_solution(7075382922398213844)
XLA Ops:
  0.0 96.8 %shard_map.28 = (bf16[2,512,1024]{2,1,0:T(8,128)(2,1)S(1)}, bf16[16,2,2,128,1024]{4,3,2,1,0:T(8,128)(2,1)S(1)}, f32[16,256,512]{2,1,0:T(8,128)S(1)}) custom-call(f32[512,1024]{1,0:T(8,128)} %geno_hbm.1, s32[512,1024]{1,0:T(8,128)} %obs_hbm.1), custom_call_target="tpu_custom_call" | custom-call | tf_op jit(solution)/shard_map/pallas_call | solution.py:395
  96.8 3.5 %shard_map.29 = f32[16,1,256,512]{3,2,1,0:T(8,128)} custom-call(bf16[16,2,2,128,1024]{4,3,2,1,0:T(8,128)(2,1)S(1)} %get-tuple-element.8.rows, bf16[2,512,1024]{2,1,0:T(8,128)(2,1)S(1)} %get-tuple-element.9.panel, f32[16,256,512]{2,1,0:T(8,128)S(1)} %get-tuple-element.10.tiles), custom_call_target="tpu_custom_call" | custom-call | tf_op jit(solution)/shard_map/pallas_call | solution.py:419
where the time goes:
time: 101 us; the launch traced here: 100 us
  Pallas kernels  100 us (99%)
    pallas_call x1, Pallas kernels, body(): pl.pallas_call(functools.partial(kernel, shards, groups), out_shape=(pltp...  96.8 us
    pallas_call x1, Pallas kernels, body(): pl.pallas_call(functools.partial(finish, shards, groups), out_shape=jax.S...  3.47 us

commit v1 on v0

--- a/solution.py
+++ b/solution.py
@@ -1,4 +1,5 @@
 import functools
+import math
 
 import jax
 import jax.numpy as jnp
@@ -16,6 +17,10 @@
 VMEM_ALL = 67043328
 VMEM_SPARE = 512 * 1024
 VMEM_FINISH = 12 * 1024 * 1024
+FOLDED_SPARE = 1024 * 1024
+FOLDED_FINISH = 8 * 1024 * 1024
+CODE_TOP = 32767.0
+TINY = 1e-30
 
 
 def index(at_z, at_y, at_core):
@@ -384,10 +389,482 @@
     lax.fori_loop(0, depth * groups * PIECES, drain, 0)
 
 
+def shape_of_line(depth):
+    z = lax.axis_index("samp") // 4
+    low = z < depth // 2
+    inward = jnp.where(low, z + 1, z - 1)
+    outward = jnp.clip(jnp.where(low, z - 1, z + 1), 0, depth - 1)
+    is_end = (z == 0) | (z == depth - 1)
+    return z, inward, outward, is_end
+
+
+def folded_finish(shards, groups, rows, panel, tiles, codes, steps, out_ref, late, out_sem):
+    depth = shards // 4
+    me = lax.axis_index("samp")
+    y = (me // 2) % 2
+    z, inward, outward, is_end = shape_of_line(depth)
+    far_mid, far_end = depth - 1 - inward, depth - 1 - z
+    last_part = lax.rem(lax.axis_index("snp") + groups - 1, groups)
+    piece_rows = rows.shape[3]
+    tile_rows = PIECES * piece_rows
+
+    def is_late(q):
+        return is_end & ((q // 4 == far_end) | ((q // 4 == far_mid) & ((q // 2) % 2 != y)))
+
+    def put(q, carry):
+        @pl.when(jnp.logical_not(is_late(q)))
+        def _():
+            pltpu.make_async_copy(tiles.at[q], out_ref.at[q, 0], out_sem.at[0]).start()
+
+        return carry
+
+    lax.fori_loop(0, shards, put, 0)
+
+    @pl.when(is_end)
+    def _():
+        def decode(t, carry):
+            for p in range(PIECES):
+                for k in range(groups):
+                    unit = (t * PIECES + p) * groups + k
+                    late[t, p * piece_rows:(p + 1) * piece_rows, k * tile_rows:(k + 1) * tile_rows] = (
+                        codes[unit].astype(jnp.float32) * steps[unit])
+            q = index(far_end, jnp.where(t // 2 == 0, y, 1 - y), lax.rem(t, 2))
+            pltpu.make_async_copy(late.at[t], out_ref.at[q, 0], out_sem.at[0]).start()
+            return carry
+
+        lax.fori_loop(0, 4, decode, 0)
+
+        def form(i, carry):
+            q = index(far_mid, 1 - y, i)
+            late[4 + i] = tiles[q] + product(rows, panel, q, [last_part])
+            pltpu.make_async_copy(late.at[4 + i], out_ref.at[q, 0], out_sem.at[0]).start()
+            return carry
+
+        lax.fori_loop(0, 2, form, 0)
+
+    pltpu.make_async_copy(tiles, out_ref.at[:, 0], out_sem.at[0]).wait()
+
+
+def folded(shards, groups, geno_hbm, obs_hbm, panel, rows, tiles, codes, steps, geno_ref, obs_ref, counts, columns,
+           made, made_steps, load_sem, count_sem, across_send, across_recv, line_send, side_send, core_send, row_recv,
+           core_recv, code_sem):
+    row_count, snp_count = geno_ref.shape
+    tile_rows = row_count // groups
+    piece_rows = tile_rows // PIECES
+    depth = shards // 4
+    me = lax.axis_index("samp")
+    part = lax.axis_index("snp")
+    y, core = (me // 2) % 2, me % 2
+    z, inward, outward, is_end = shape_of_line(depth)
+    other = lax.rem(part + 1, groups)
+    load_rows = row_count // LOADS
+
+    def load(i):
+        block = pl.ds(pl.multiple_of(i * load_rows, load_rows), load_rows)
+        return (pltpu.make_async_copy(geno_hbm.at[block], geno_ref.at[block], load_sem.at[0, i]),
+                pltpu.make_async_copy(obs_hbm.at[block], obs_ref.at[block], load_sem.at[1, i]))
+
+    for i in range(LOADS):
+        for copy in load(i):
+            copy.start()
+
+    barrier = pltpu.get_barrier_semaphore()
+    for step in range(1, shards):
+        pl.semaphore_signal(barrier, inc=1, device_id={"samp": lax.rem(me + step, shards)}, device_id_type=MESH)
+    pl.semaphore_signal(barrier, inc=1, device_id={"snp": other}, device_id_type=MESH)
+
+    def add_strip(i, total):
+        alt, call = total
+        strip = pl.ds(pl.multiple_of(i * STRIP, STRIP), STRIP)
+        present = obs_ref[strip, :].astype(jnp.float32)
+        held = present * geno_ref[strip, :]
+        for r in range(0, STRIP, 8):
+            alt = alt + held[r:r + 8]
+            call = call + present[r:r + 8]
+        return alt, call
+
+    zero = jnp.zeros((8, snp_count), jnp.float32)
+    alt, call = zero, zero
+    strips = load_rows // STRIP
+    for i in range(LOADS):
+        for copy in load(i):
+            copy.wait()
+        alt, call = lax.fori_loop(i * strips, (i + 1) * strips, add_strip, (alt, call))
+    counts[me, 0:1, :] = jnp.sum(alt, axis=0, keepdims=True)
+    counts[me, 1:2, :] = jnp.sum(call, axis=0, keepdims=True)
+
+    pl.semaphore_wait(barrier, shards)
+
+    for step in range(1, shards):
+        pltpu.make_async_remote_copy(
+            src_ref=counts.at[me], dst_ref=counts.at[me], send_sem=count_sem.at[0], recv_sem=count_sem.at[1],
+            device_id={"samp": lax.rem(me + step, shards)}, device_id_type=MESH).start()
+
+    def await_bytes(ref, sem):
+        pltpu.make_async_copy(ref, ref, sem).wait()
+
+    others = counts.at[pl.ds(0, shards - 1)]
+    await_bytes(others, count_sem.at[1])
+    sums = counts[0]
+    for s in range(1, shards):
+        sums = sums + counts[s]
+    frequency = sums[0:1] / (2.0 * jnp.maximum(sums[1:2], 1.0))
+    shift = 2.0 * frequency
+    gain = lax.rsqrt(jnp.maximum(shift * (1.0 - frequency), var_floor))
+
+    def piece_of(k, p):
+        return pl.ds(pl.multiple_of(k * tile_rows + p * piece_rows, piece_rows), piece_rows)
+
+    strip_rows = min(STRIP, piece_rows)
+
+    def scale_piece(k, p):
+        def scale_strip(i, carry):
+            start = pl.multiple_of(k * tile_rows + p * piece_rows + i * strip_rows, strip_rows)
+            strip = pl.ds(start, strip_rows)
+            present = obs_ref[strip, :].astype(jnp.float32)
+            panel[part, strip, :] = (present * (geno_ref[strip, :] - shift) * gain).astype(jnp.bfloat16)
+            return carry
+
+        lax.fori_loop(0, piece_rows // strip_rows, scale_strip, 0)
+
+    def panel_copy(k, p):
+        block = panel.at[part, piece_of(k, p)]
+        return pltpu.make_async_remote_copy(
+            src_ref=block, dst_ref=block, send_sem=across_send.at[0],
+            recv_sem=across_recv.at[jnp.where(k == part, PIECES, p)], device_id={"snp": other}, device_id_type=MESH)
+
+    def column_copy(q, h, p):
+        return pltpu.make_async_remote_copy(
+            src_ref=rows.at[q, h, p], dst_ref=columns.at[part, h, pl.ds(pl.multiple_of(p * piece_rows, piece_rows), piece_rows)],
+            send_sem=across_send.at[1], recv_sem=across_recv.at[PIECES + 1], device_id={"snp": other}, device_id_type=MESH)
+
+    def own_copy(q, h, p, to, send_sem, src):
+        return pltpu.make_async_remote_copy(
+            src_ref=rows.at[q, h, p] if src is None else src, dst_ref=rows.at[q, h, p], send_sem=send_sem,
+            recv_sem=row_recv.at[q // 2, h, p], device_id={"samp": to}, device_id_type=MESH)
+
+    def send_in(q, h, p, src=None, extra=0):
+        own_copy(q, h, p, index(inward, y, core), line_send.at[extra], src).start()
+
+    def send_out(q, h, p, src=None):
+        own_copy(q, h, p, index(outward, y, core), line_send.at[2], src).start()
+
+    def send_side(q, h, p, src=None, extra=0):
+        own_copy(q, h, p, index(z, 1 - y, core), side_send.at[extra], src).start()
+
+    def half_of(q, h, p):
+        return jnp.where(jnp.logical_not(is_end) & (q // 4 == depth - 1 - outward), p, h)
+
+    def send_core(q, h, p, src=None):
+        pltpu.make_async_remote_copy(
+            src_ref=rows.at[q, h, p] if src is None else src, dst_ref=rows.at[q, h, p], send_sem=core_send.at[0],
+            recv_sem=core_recv.at[q // 2, half_of(q, h, p)], device_id={"samp": index(z, y, 1 - core)},
+            device_id_type=MESH).start()
+
+    def arrive(q, h, p):
+        await_bytes(rows.at[q, h, p], row_recv.at[q // 2, h, p])
+
+    def arrive_core(q, half):
+        await_bytes(rows.at[q, 0], core_recv.at[q // 2, half])
+
+    def part_at(i):
+        return lax.rem(part + i, groups)
+
+    def send_own(h, p):
+        mine = panel.at[h, piece_of(part, p)]
+        send_side(me, h, p, mine)
+        send_in(me, h, p, mine)
+
+        @pl.when(jnp.logical_not(is_end))
+        def _():
+            send_out(me, h, p, mine)
+
+        send_core(me, h, p, mine)
+        rows[me, h, p] = panel[h, piece_of(part, p), :]
+
+    for p in range(PIECES):
+        scale_piece(other, p)
+        panel_copy(other, p).start()
+        scale_piece(part, p)
+        send_own(part, p)
+    for p in range(PIECES):
+        panel_copy(part, p).start()
+    for p in range(PIECES):
+        await_bytes(panel.at[other, piece_of(part, p)], across_recv.at[p])
+        send_own(other, p)
+
+    def form(at_z, at_y, parts=None, wait=True):
+        def per_core(t, carry):
+            q = index(at_z, at_y, lax.rem(core + t, 2))
+            if wait:
+                @pl.when(t == 1)
+                def _():
+                    for half in (range(2) if parts is None else parts):
+                        arrive_core(q, half)
+
+            tiles[q] = product(rows, panel, q, range(groups) if parts is None else parts)
+            return carry
+
+        lax.fori_loop(0, 2, per_core, 0)
+
+    def await_panel():
+        await_bytes(panel.at[other, pl.ds(pl.multiple_of(other * tile_rows, tile_rows), tile_rows)], across_recv.at[PIECES])
+
+    def pick(i, values):
+        chosen = values[-1]
+        for n in range(len(values) - 2, -1, -1):
+            chosen = jnp.where(i == n, values[n], chosen)
+        return chosen
+
+    count = groups * PIECES
+
+    @pl.when(is_end)
+    def _():
+        far_mid = depth - 1 - inward
+
+        def first(t, carry):
+            h, p = part_at(t // PIECES), lax.rem(t, PIECES)
+            near, beside = index(inward, y, core), index(z, 1 - y, core)
+            arrive(near, h, p)
+            send_side(near, h, p)
+            send_core(near, h, p)
+            arrive(beside, h, p)
+            send_in(beside, h, p)
+            send_core(beside, h, p)
+            return carry
+
+        lax.fori_loop(0, count, first, 0)
+        await_panel()
+
+        def second(t, carry):
+            h, p = part_at(t // PIECES), lax.rem(t, PIECES)
+            far, cross = index(far_mid, y, core), index(inward, 1 - y, core)
+            arrive(far, h, p)
+            send_side(far, h, p)
+            send_core(far, h, p)
+            arrive(cross, h, p)
+            send_core(cross, h, p)
+
+            @pl.when(t < 3)
+            def _():
+                form(pick(t, (z, inward, z)), pick(t, (y, y, 1 - y)))
+
+            return carry
+
+        lax.fori_loop(0, count, second, 0)
+
+        def third(t, carry):
+            h, p = part_at(t // PIECES), lax.rem(t, PIECES)
+            q = index(far_mid, 1 - y, core)
+            arrive(q, h, p)
+            send_core(q, h, p)
+
+            @pl.when(t < 2)
+            def _():
+                form(pick(t, (far_mid, inward)), pick(t, (y, 1 - y)))
+
+            @pl.when(t == 2)
+            def _():
+                form(far_mid, 1 - y, [part])
+
+            return carry
+
+        lax.fori_loop(0, count, third, 0)
+        await_bytes(codes, code_sem.at[1])
+        await_bytes(steps, code_sem.at[3])
+        arrive_core(index(far_mid, 1 - y, 1 - core), other)
+        await_bytes(rows.at[pl.ds(0, 2)], line_send.at[0])
+        await_bytes(rows.at[pl.ds(0, 3)], side_send.at[0])
+        await_bytes(rows.at[pl.ds(0, 6)], core_send.at[0])
+
+    @pl.when(jnp.logical_not(is_end))
+    def _():
+        far = depth - 1 - outward
+
+        def first(t, carry):
+            h, p = part_at(t // PIECES), lax.rem(t, PIECES)
+            end, near, beside = index(outward, y, core), index(inward, y, core), index(z, 1 - y, core)
+            arrive(end, h, p)
+            send_in(end, h, p)
+            send_core(end, h, p)
+            column_copy(end, h, p).start()
+            arrive(near, h, p)
+            send_out(near, h, p)
+            send_core(near, h, p)
+            arrive(beside, h, p)
+            send_core(beside, h, p)
+            return carry
+
+        lax.fori_loop(0, count, first, 0)
+        for p in range(PIECES):
+            send_in(index(z, 1 - y, core), part, p, extra=1)
+        for h in range(groups):
+            columns[part, h] = rows[index(outward, y, core), h].reshape(tile_rows, snp_count)
+        await_panel()
+
+        def make(side, p, k):
+            def per_core(t, carry):
+                which = lax.rem(core + t, 2)
+                q = index(far, jnp.where(side == 0, y, 1 - y), which)
+                term = None
+                for h in range(groups):
+                    one = lax.dot_general(rows[q, h, p], columns[k, h], (((1,), (1,)), ((), ())),
+                                          preferred_element_type=jnp.float32)
+                    term = one if term is None else term + one
+                term = term * (1.0 / (groups * snp_count))
+                top = jnp.max(jnp.abs(term), axis=0, keepdims=True)
+                unit = ((side * 2 + which) * PIECES + p) * groups + k
+                made[unit] = jnp.round(term * (CODE_TOP / jnp.maximum(top, TINY))).astype(jnp.int32).astype(jnp.int16)
+                made_steps[unit] = top * (1.0 / CODE_TOP)
+                for n, (source, target) in enumerate(((made, codes), (made_steps, steps))):
+                    pltpu.make_async_remote_copy(
+                        src_ref=source.at[unit], dst_ref=target.at[unit], send_sem=code_sem.at[2 * n],
+                        recv_sem=code_sem.at[2 * n + 1], device_id={"samp": index(outward, y, core)},
+                        device_id_type=MESH).start()
+                return carry
+
+            lax.fori_loop(0, 2, per_core, 0)
+
+        def far_core(side, p):
+            arrive_core(index(far, jnp.where(side == 0, y, 1 - y), 1 - core), p)
+
+        def make_list(listed):
+            def per_entry(i, carry):
+                side, p, away = (pick(i, [entry[n] for entry in listed]) for n in range(3))
+                make(side, p, lax.rem(part + away, groups))
+                return carry
+
+            lax.fori_loop(0, len(listed), per_entry, 0)
+
+        def second(t, carry):
+            h, p = part_at(lax.rem(t, groups)), t // groups
+            far_q, cross = index(far, y, core), index(outward, 1 - y, core)
+
+            @pl.when(t == 3)
+            def _():
+                far_core(0, 0)
+                far_core(1, 0)
+                make_list([(0, 0, 0), (1, 0, 0)])
+
+            arrive(far_q, h, p)
+            send_side(far_q, h, p)
+            send_core(far_q, h, p)
+            ch, cp = part_at(t // PIECES), lax.rem(t, PIECES)
+            arrive(cross, ch, cp)
+            send_core(cross, ch, cp)
+
+            @pl.when(t > 0)
+            def _():
+                q = index(far, 1 - y, core)
+                h, p = part_at(lax.rem(t - 1, groups)), (t - 1) // groups
+                arrive(q, h, p)
+                send_core(q, h, p)
+
+            form(pick(t, (z, outward, inward, z)), pick(t, (y, y, y, 1 - y)))
+            return carry
+
+        lax.fori_loop(0, count, second, 0)
+        for p in range(PIECES):
+            send_side(index(inward, y, core), other, p, extra=1)
+        far_core(0, 1)
+        make_list([(0, 1, 0)])
+        await_bytes(columns.at[other], across_recv.at[PIECES + 1])
+        make_list([(0, 0, 1), (0, 1, 1), (1, 0, 1)])
+        q = index(far, 1 - y, core)
+        arrive(q, other, PIECES - 1)
+        send_core(q, other, PIECES - 1)
+        far_core(1, 1)
+        make_list([(1, 1, 0), (1, 1, 1)])
+
+        def third(t, carry):
+            h, p = part_at(t // PIECES), lax.rem(t, PIECES)
+            q = index(inward, 1 - y, core)
+            arrive(q, h, p)
+            send_core(q, h, p)
+
+            @pl.when(t == 0)
+            def _():
+                form(outward, 1 - y)
+
+            return carry
+
+        lax.fori_loop(0, count, third, 0)
+        form(far, y, wait=False)
+        form(far, 1 - y, wait=False)
+        form(inward, 1 - y)
+        await_bytes(rows.at[pl.ds(0, 2)], line_send.at[0])
+        await_bytes(rows.at[0, 0], line_send.at[1])
+        await_bytes(rows.at[pl.ds(0, 2)], line_send.at[2])
+        await_bytes(rows.at[pl.ds(0, 2)], side_send.at[0])
+        await_bytes(rows.at[0, 0], side_send.at[1])
+        await_bytes(rows.at[pl.ds(0, 8)], core_send.at[0])
+        await_bytes(rows.at[0], across_send.at[1])
+        await_bytes(made, code_sem.at[0])
+        await_bytes(made_steps, code_sem.at[2])
+
+    await_bytes(others, count_sem.at[0])
+    await_bytes(rows.at[0], across_send.at[0])
+
+
+def folded_body(shards, groups, genotypes, observed):
+    row_count, snp_count = genotypes.shape
+    tile_rows = row_count // groups
+    piece_rows = tile_rows // PIECES
+    units = 4 * PIECES * groups
+    outs = (
+        pltpu.VMEM((groups, row_count, snp_count), jnp.bfloat16),
+        pltpu.VMEM((shards, groups, PIECES, piece_rows, snp_count), jnp.bfloat16),
+        pltpu.VMEM((shards, tile_rows, row_count), jnp.float32),
+        pltpu.VMEM((units, piece_rows, tile_rows), jnp.int16),
+        pltpu.VMEM((units, 1, tile_rows), jnp.float32),
+    )
+    kept = sum(math.prod(o.shape) * jnp.dtype(o.dtype).itemsize for o in outs)
+    held = pl.pallas_call(
+        functools.partial(folded, shards, groups),
+        out_shape=outs,
+        in_specs=[pl.BlockSpec(memory_space=pltpu.HBM)] * 2,
+        out_specs=[pl.BlockSpec(memory_space=pltpu.VMEM)] * 5,
+        scratch_shapes=[
+            pltpu.VMEM((row_count, snp_count), jnp.float32),
+            pltpu.VMEM((row_count, snp_count), jnp.int32),
+            pltpu.VMEM((shards, 2, snp_count), jnp.float32),
+            pltpu.VMEM((groups, groups, tile_rows, snp_count), jnp.bfloat16),
+            pltpu.VMEM((units, piece_rows, tile_rows), jnp.int16),
+            pltpu.VMEM((units, 1, tile_rows), jnp.float32),
+            pltpu.SemaphoreType.DMA((2, LOADS)),
+            pltpu.SemaphoreType.DMA((2,)),
+            pltpu.SemaphoreType.DMA((2,)),
+            pltpu.SemaphoreType.DMA((PIECES + 2,)),
+            pltpu.SemaphoreType.DMA((3,)),
+            pltpu.SemaphoreType.DMA((2,)),
+            pltpu.SemaphoreType.DMA((1,)),
+            pltpu.SemaphoreType.DMA((shards // 2, groups, PIECES)),
+            pltpu.SemaphoreType.DMA((shards // 2, 2)),
+            pltpu.SemaphoreType.DMA((4,)),
+        ],
+        compiler_params=pltpu.CompilerParams(
+            collective_id=0, has_side_effects=True, vmem_limit_bytes=VMEM_ALL - FOLDED_SPARE - kept),
+    )(genotypes, observed)
+    panel, rows, tiles, codes, steps = held
+    return pl.pallas_call(
+        functools.partial(folded_finish, shards, groups),
+        out_shape=jax.ShapeDtypeStruct((shards, 1, tile_rows, row_count), jnp.float32),
+        in_specs=[pl.BlockSpec(memory_space=pltpu.VMEM)] * 5,
+        out_specs=pl.BlockSpec(memory_space=pltpu.HBM),
+        scratch_shapes=[
+            pltpu.VMEM((6, tile_rows, row_count), jnp.float32),
+            pltpu.SemaphoreType.DMA((1,)),
+        ],
+        compiler_params=pltpu.CompilerParams(vmem_limit_bytes=FOLDED_FINISH),
+    )(rows, panel, tiles, codes, steps)
+
+
 def solution(mesh):
     shards, groups = mesh.shape["samp"], mesh.shape["snp"]
 
     def body(genotypes, observed):
+        if groups == 2 and shards == 16:
+            return folded_body(shards, groups, genotypes, observed)
         row_count, snp_count = genotypes.shape
         tile_rows = row_count // groups
         piece_rows = tile_rows // PIECES

time: 101 us -> 91.8 us (0.909)
  Pallas kernels: 100 us -> 91.6 us
    pallas_call x2, Pallas kernels: 100 us -> 91.6 us  [the longest x1 88.3 us: folded_body(): pl.pallas_call(functools.partial(folded, shards, groups), out_shape=outs,...]
where the time goes in v1:
time: 91.8 us; the launch traced here: 91.6 us
  Pallas kernels  91.6 us (100%)
    pallas_call x1, Pallas kernels, folded_body(): pl.pallas_call(functools.partial(folded, shards, groups), out_shape=outs,...  88.3 us
    pallas_call x1, Pallas kernels, folded_body(): pl.pallas_call(functools.partial(folded_finish, shards, groups), out_shap...  3.32 us

profile of v1, /device:TPU:0, one launch (start us, length us, event | category | flops | bytes accessed | tf_op | source)
XLA Modules:
  0.0 91.6 jit_solution(13588525654057888784)
XLA Ops:
  0.0 88.3 %shard_map.28 = (bf16[2,512,1024]{2,1,0:T(8,128)(2,1)S(1)}, bf16[16,2,2,128,1024]{4,3,2,1,0:T(8,128)(2,1)S(1)}, f32[16,256,512]{2,1,0:T(8,128)S(1)}, s16[16,128,256]{2,1,0:T(8,128)(2,1)S(1)}, f32[16,1,256]{2,1,0:T(1,128)S(1)}) custom-call(f32[512,1024]{1,0:T(8,128)} %geno_hbm.1, s32[512,1024]{1,0:T(8,128)} %obs_hbm.1), custom_call_target="tpu_custom_call" | custom-call | tf_op jit(solution)/shard_map/pallas_call | solution.py:822
  88.3 3.3 %shard_map.29 = f32[16,1,256,512]{3,2,1,0:T(8,128)} custom-call(bf16[16,2,2,128,1024]{4,3,2,1,0:T(8,128)(2,1)S(1)} %get-tuple-element.10.rows, bf16[2,512,1024]{2,1,0:T(8,128)(2,1)S(1)} %get-tuple-element.11.panel, f32[16,256,512]{2,1,0:T(8,128)S(1)} %get-tuple-element.12.tiles, s16[16,128,256]{2,1,0:T(8,128)(2,1)S(1)} %get-tuple-element.13.codes, ...), custom_call_target="tpu_custom_call" | custom-call | tf_op jit(solution)/shard_map/pallas_call | solution.py:849

commit v2 on v1

--- a/solution.py
+++ b/solution.py
@@ -685,7 +685,15 @@
             h, p = part_at(t // PIECES), lax.rem(t, PIECES)
             end, near, beside = index(outward, y, core), index(inward, y, core), index(z, 1 - y, core)
             arrive(end, h, p)
-            send_in(end, h, p)
+
+            @pl.when(p == 0)
+            def _():
+                send_in(end, h, 0)
+
+            @pl.when(h == other)
+            def _():
+                send_in(end, jnp.where(p == 0, part, other), 1)
+
             send_core(end, h, p)
             column_copy(end, h, p).start()
             arrive(near, h, p)
@@ -740,11 +748,10 @@
             h, p = part_at(lax.rem(t, groups)), t // groups
             far_q, cross = index(far, y, core), index(outward, 1 - y, core)
 
-            @pl.when(t == 3)
-            def _():
-                far_core(0, 0)
-                far_core(1, 0)
-                make_list([(0, 0, 0), (1, 0, 0)])
+            @pl.when(t >= 2)
+            def _():
+                far_core(t - 2, 0)
+                make(t - 2, 0, part)
 
             arrive(far_q, h, p)
             send_side(far_q, h, p)
@@ -770,6 +777,7 @@
         make_list([(0, 1, 0)])
         await_bytes(columns.at[other], across_recv.at[PIECES + 1])
         make_list([(0, 0, 1), (0, 1, 1), (1, 0, 1)])
+        form(outward, 1 - y)
         q = index(far, 1 - y, core)
         arrive(q, other, PIECES - 1)
         send_core(q, other, PIECES - 1)
@@ -782,15 +790,13 @@
             arrive(q, h, p)
             send_core(q, h, p)
 
-            @pl.when(t == 0)
-            def _():
-                form(outward, 1 - y)
+            @pl.when(t < 2)
+            def _():
+                form(far, pick(t, (y, 1 - y)), wait=False)
 
             return carry
 
         lax.fori_loop(0, count, third, 0)
-        form(far, y, wait=False)
-        form(far, 1 - y, wait=False)
         form(inward, 1 - y)
         await_bytes(rows.at[pl.ds(0, 2)], line_send.at[0])
         await_bytes(rows.at[0, 0], line_send.at[1])

time: 91.8 us -> 85.4 us (0.930)
  Pallas kernels: 91.6 us -> 85.2 us
    pallas_call x1, Pallas kernels: 88.3 us -> 81.9 us  [folded_body(): pl.pallas_call(functools.partial(folded, shards, groups), out_shape=outs,...]
where the time goes in v2:
time: 85.4 us; the launch traced here: 85.3 us
  Pallas kernels  85.2 us (100%)
    pallas_call x1, Pallas kernels, folded_body(): pl.pallas_call(functools.partial(folded, shards, groups), out_shape=outs,...  81.9 us
    pallas_call x1, Pallas kernels, folded_body(): pl.pallas_call(functools.partial(folded_finish, shards, groups), out_shap...  3.32 us

profile of v2, /device:TPU:0, one launch (start us, length us, event | category | flops | bytes accessed | tf_op | source)
XLA Modules:
  0.0 85.3 jit_solution(9144586687702937263)
XLA Ops:
  0.0 81.9 %shard_map.28 = (bf16[2,512,1024]{2,1,0:T(8,128)(2,1)S(1)}, bf16[16,2,2,128,1024]{4,3,2,1,0:T(8,128)(2,1)S(1)}, f32[16,256,512]{2,1,0:T(8,128)S(1)}, s16[16,128,256]{2,1,0:T(8,128)(2,1)S(1)}, f32[16,1,256]{2,1,0:T(1,128)S(1)}) custom-call(f32[512,1024]{1,0:T(8,128)} %geno_hbm.1, s32[512,1024]{1,0:T(8,128)} %obs_hbm.1), custom_call_target="tpu_custom_call" | custom-call | tf_op jit(solution)/shard_map/pallas_call | solution.py:828
  81.9 3.3 %shard_map.29 = f32[16,1,256,512]{3,2,1,0:T(8,128)} custom-call(bf16[16,2,2,128,1024]{4,3,2,1,0:T(8,128)(2,1)S(1)} %get-tuple-element.10.rows, bf16[2,512,1024]{2,1,0:T(8,128)(2,1)S(1)} %get-tuple-element.11.panel, f32[16,256,512]{2,1,0:T(8,128)S(1)} %get-tuple-element.12.tiles, s16[16,128,256]{2,1,0:T(8,128)(2,1)S(1)} %get-tuple-element.13.codes, ...), custom_call_target="tpu_custom_call" | custom-call | tf_op jit(solution)/shard_map/pallas_call | solution.py:855

commit v3 on v2

--- a/solution.py
+++ b/solution.py
@@ -495,10 +495,14 @@
 
     pl.semaphore_wait(barrier, shards)
 
-    for step in range(1, shards):
-        pltpu.make_async_remote_copy(
-            src_ref=counts.at[me], dst_ref=counts.at[me], send_sem=count_sem.at[0], recv_sem=count_sem.at[1],
-            device_id={"samp": lax.rem(me + step, shards)}, device_id_type=MESH).start()
+    for step in range(shards):
+        to = jnp.where(z < depth // 2, shards - 1 - step, step)
+
+        @pl.when(to != me)
+        def _():
+            pltpu.make_async_remote_copy(
+                src_ref=counts.at[me], dst_ref=counts.at[me], send_sem=count_sem.at[0], recv_sem=count_sem.at[1],
+                device_id={"samp": to}, device_id_type=MESH).start()
 
     def await_bytes(ref, sem):
         pltpu.make_async_copy(ref, ref, sem).wait()
@@ -538,6 +542,14 @@
             src_ref=rows.at[q, h, p], dst_ref=columns.at[part, h, pl.ds(pl.multiple_of(p * piece_rows, piece_rows), piece_rows)],
             send_sem=across_send.at[1], recv_sem=across_recv.at[PIECES + 1], device_id={"snp": other}, device_id_type=MESH)
 
+    cut = piece_rows * 7 // 8
+    head, rest = pl.ds(0, cut), pl.ds(cut, piece_rows - cut)
+
+    def span_copy(q, h, p, span, to, send_sem, recv_sem):
+        return pltpu.make_async_remote_copy(
+            src_ref=rows.at[q, h, p, span], dst_ref=rows.at[q, h, p, span], send_sem=send_sem, recv_sem=recv_sem,
+            device_id={"samp": to}, device_id_type=MESH)
+
     def own_copy(q, h, p, to, send_sem, src):
         return pltpu.make_async_remote_copy(
             src_ref=rows.at[q, h, p] if src is None else src, dst_ref=rows.at[q, h, p], send_sem=send_sem,
@@ -561,6 +573,9 @@
             recv_sem=core_recv.at[q // 2, half_of(q, h, p)], device_id={"samp": index(z, y, 1 - core)},
             device_id_type=MESH).start()
 
+    def send_core_span(q, h, p, span):
+        span_copy(q, h, p, span, index(z, y, 1 - core), core_send.at[0], core_recv.at[q // 2, half_of(q, h, p)]).start()
+
     def arrive(q, h, p):
         await_bytes(rows.at[q, h, p], row_recv.at[q // 2, h, p])
 
@@ -583,10 +598,10 @@
         rows[me, h, p] = panel[h, piece_of(part, p), :]
 
     for p in range(PIECES):
+        scale_piece(part, p)
+        send_own(part, p)
         scale_piece(other, p)
         panel_copy(other, p).start()
-        scale_piece(part, p)
-        send_own(part, p)
     for p in range(PIECES):
         panel_copy(part, p).start()
     for p in range(PIECES):
@@ -640,7 +655,20 @@
             h, p = part_at(t // PIECES), lax.rem(t, PIECES)
             far, cross = index(far_mid, y, core), index(inward, 1 - y, core)
             arrive(far, h, p)
-            send_side(far, h, p)
+            to = index(z, 1 - y, core)
+
+            @pl.when(p == 0)
+            def _():
+                send_side(far, h, p, extra=1)
+
+            @pl.when(p == 1)
+            def _():
+                span_copy(far, h, p, head, to, side_send.at[1], row_recv.at[far // 2, h, p]).start()
+
+            @pl.when((p == 1) & (h == other))
+            def _():
+                span_copy(far, h, p, rest, to, side_send.at[1], code_sem.at[5]).start()
+
             send_core(far, h, p)
             arrive(cross, h, p)
             send_core(cross, h, p)
@@ -656,8 +684,16 @@
         def third(t, carry):
             h, p = part_at(t // PIECES), lax.rem(t, PIECES)
             q = index(far_mid, 1 - y, core)
-            arrive(q, h, p)
-            send_core(q, h, p)
+
+            @pl.when(p == 0)
+            def _():
+                arrive(q, h, p)
+                send_core(q, h, p)
+
+            @pl.when(p == 1)
+            def _():
+                await_bytes(rows.at[q, h, p, head], row_recv.at[q // 2, h, p])
+                send_core_span(q, h, p, head)
 
             @pl.when(t < 2)
             def _():
@@ -665,16 +701,24 @@
 
             @pl.when(t == 2)
             def _():
-                form(far_mid, 1 - y, [part])
+                await_bytes(rows.at[q, part, 1, rest], code_sem.at[4])
+                send_core_span(q, part, 1, rest)
+
+            @pl.when(t == 3)
+            def _():
+                await_bytes(rows.at[q, other, 1, rest], code_sem.at[5])
+                send_core_span(q, other, 1, rest)
 
             return carry
 
         lax.fori_loop(0, count, third, 0)
+        form(far_mid, 1 - y, [part])
         await_bytes(codes, code_sem.at[1])
         await_bytes(steps, code_sem.at[3])
         arrive_core(index(far_mid, 1 - y, 1 - core), other)
         await_bytes(rows.at[pl.ds(0, 2)], line_send.at[0])
-        await_bytes(rows.at[pl.ds(0, 3)], side_send.at[0])
+        await_bytes(rows.at[pl.ds(0, 2)], side_send.at[0])
+        await_bytes(geno_ref.at[pl.ds(0, (count * piece_rows - (piece_rows - cut)) // 2)], side_send.at[1])
         await_bytes(rows.at[pl.ds(0, 6)], core_send.at[0])
 
     @pl.when(jnp.logical_not(is_end))
@@ -781,14 +825,18 @@
         q = index(far, 1 - y, core)
         arrive(q, other, PIECES - 1)
         send_core(q, other, PIECES - 1)
-        far_core(1, 1)
-        make_list([(1, 1, 0), (1, 1, 1)])
+        cross = index(inward, 1 - y, core)
 
         def third(t, carry):
             h, p = part_at(t // PIECES), lax.rem(t, PIECES)
-            q = index(inward, 1 - y, core)
-            arrive(q, h, p)
-            send_core(q, h, p)
+            arrive(cross, h, p)
+            send_core(cross, h, p)
+
+            @pl.when(t == 1)
+            def _():
+                span_copy(cross, h, p, rest, index(outward, y, core), line_send.at[3], code_sem.at[4]).start()
+                far_core(1, 1)
+                make_list([(1, 1, 0), (1, 1, 1)])
 
             @pl.when(t < 2)
             def _():
@@ -801,6 +849,7 @@
         await_bytes(rows.at[pl.ds(0, 2)], line_send.at[0])
         await_bytes(rows.at[0, 0], line_send.at[1])
         await_bytes(rows.at[pl.ds(0, 2)], line_send.at[2])
+        await_bytes(geno_ref.at[pl.ds(0, (piece_rows - cut) // 2)], line_send.at[3])
         await_bytes(rows.at[pl.ds(0, 2)], side_send.at[0])
         await_bytes(rows.at[0, 0], side_send.at[1])
         await_bytes(rows.at[pl.ds(0, 8)], core_send.at[0])
@@ -841,12 +890,12 @@
             pltpu.SemaphoreType.DMA((2,)),
             pltpu.SemaphoreType.DMA((2,)),
             pltpu.SemaphoreType.DMA((PIECES + 2,)),
-            pltpu.SemaphoreType.DMA((3,)),
+            pltpu.SemaphoreType.DMA((4,)),
             pltpu.SemaphoreType.DMA((2,)),
             pltpu.SemaphoreType.DMA((1,)),
             pltpu.SemaphoreType.DMA((shards // 2, groups, PIECES)),
             pltpu.SemaphoreType.DMA((shards // 2, 2)),
-            pltpu.SemaphoreType.DMA((4,)),
+            pltpu.SemaphoreType.DMA((6,)),
         ],
         compiler_params=pltpu.CompilerParams(
             collective_id=0, has_side_effects=True, vmem_limit_bytes=VMEM_ALL - FOLDED_SPARE - kept),

time: 85.4 us -> 84.9 us (level)
  no operation moved by 1% of the time
where the time goes in v3:
time: 84.9 us; the launch traced here: 84.8 us
  Pallas kernels  84.8 us (100%)
    pallas_call x1, Pallas kernels, folded_body(): pl.pallas_call(functools.partial(folded, shards, groups), out_shape=outs,...  81.5 us
    pallas_call x1, Pallas kernels, folded_body(): pl.pallas_call(functools.partial(folded_finish, shards, groups), out_shap...  3.32 us

profile of v3, /device:TPU:0, one launch (start us, length us, event | category | flops | bytes accessed | tf_op | source)
XLA Modules:
  0.0 84.8 jit_solution(9961414700778667272)
XLA Ops:
  0.0 81.5 %shard_map.28 = (bf16[2,512,1024]{2,1,0:T(8,128)(2,1)S(1)}, bf16[16,2,2,128,1024]{4,3,2,1,0:T(8,128)(2,1)S(1)}, f32[16,256,512]{2,1,0:T(8,128)S(1)}, s16[16,128,256]{2,1,0:T(8,128)(2,1)S(1)}, f32[16,1,256]{2,1,0:T(1,128)S(1)}) custom-call(f32[512,1024]{1,0:T(8,128)} %geno_hbm.1, s32[512,1024]{1,0:T(8,128)} %obs_hbm.1), custom_call_target="tpu_custom_call" | custom-call | tf_op jit(solution)/shard_map/pallas_call | solution.py:877
  81.5 3.3 %shard_map.29 = f32[16,1,256,512]{3,2,1,0:T(8,128)} custom-call(bf16[16,2,2,128,1024]{4,3,2,1,0:T(8,128)(2,1)S(1)} %get-tuple-element.10.rows, bf16[2,512,1024]{2,1,0:T(8,128)(2,1)S(1)} %get-tuple-element.11.panel, f32[16,256,512]{2,1,0:T(8,128)S(1)} %get-tuple-element.12.tiles, s16[16,128,256]{2,1,0:T(8,128)(2,1)S(1)} %get-tuple-element.13.codes, ...), custom_call_target="tpu_custom_call" | custom-call | tf_op jit(solution)/shard_map/pallas_call | solution.py:904

commit v4 on v3

--- a/solution.py
+++ b/solution.py
@@ -21,6 +21,7 @@
 FOLDED_FINISH = 8 * 1024 * 1024
 CODE_TOP = 32767.0
 TINY = 1e-30
+RAW = 32
 
 
 def index(at_z, at_y, at_core):
@@ -446,8 +447,8 @@
 
 
 def folded(shards, groups, geno_hbm, obs_hbm, panel, rows, tiles, codes, steps, geno_ref, obs_ref, counts, columns,
-           made, made_steps, load_sem, count_sem, across_send, across_recv, line_send, side_send, core_send, row_recv,
-           core_recv, code_sem):
+           made, made_steps, raw, raw_in, load_sem, count_sem, across_send, across_recv, line_send, side_send, core_send, row_recv,
+           core_recv, code_sem, raw_sem):
     row_count, snp_count = geno_ref.shape
     tile_rows = row_count // groups
     piece_rows = tile_rows // PIECES
@@ -490,8 +491,9 @@
         for copy in load(i):
             copy.wait()
         alt, call = lax.fori_loop(i * strips, (i + 1) * strips, add_strip, (alt, call))
-    counts[me, 0:1, :] = jnp.sum(alt, axis=0, keepdims=True)
-    counts[me, 1:2, :] = jnp.sum(call, axis=0, keepdims=True)
+    alt_step = 2.0 * row_count / CODE_TOP
+    both = jnp.concatenate([jnp.sum(alt, axis=0, keepdims=True) * (1.0 / alt_step), jnp.sum(call, axis=0, keepdims=True)])
+    counts[me] = jnp.round(both).astype(jnp.int32).astype(jnp.int16)
 
     pl.semaphore_wait(barrier, shards)
 
@@ -507,12 +509,29 @@
     def await_bytes(ref, sem):
         pltpu.make_async_copy(ref, ref, sem).wait()
 
+    def await_rows(count, sem):
+        await_bytes(geno_ref.at[pl.ds(0, count // 2)], sem)
+
+    def raw_copy(to, slot):
+        return pltpu.make_async_remote_copy(
+            src_ref=raw, dst_ref=raw_in.at[slot], send_sem=raw_sem.at[0], recv_sem=raw_sem.at[1 + slot],
+            device_id={"samp": to}, device_id_type=MESH)
+
+    early = pl.ds(pl.multiple_of(part * tile_rows, tile_rows), RAW)
+    raw[...] = jnp.where(obs_ref[early, :] > 0, geno_ref[early, :], -1.0)
+    raw_copy(index(z, 1 - y, core), 0).start()
+    raw_copy(index(inward, y, core), jnp.where(is_end, 2, 1)).start()
+
+    @pl.when(jnp.logical_not(is_end))
+    def _():
+        raw_copy(index(outward, y, core), 1).start()
+
     others = counts.at[pl.ds(0, shards - 1)]
     await_bytes(others, count_sem.at[1])
-    sums = counts[0]
+    sums = counts[0].astype(jnp.float32)
     for s in range(1, shards):
-        sums = sums + counts[s]
-    frequency = sums[0:1] / (2.0 * jnp.maximum(sums[1:2], 1.0))
+        sums = sums + counts[s].astype(jnp.float32)
+    frequency = sums[0:1] * alt_step / (2.0 * jnp.maximum(sums[1:2], 1.0))
     shift = 2.0 * frequency
     gain = lax.rsqrt(jnp.maximum(shift * (1.0 - frequency), var_floor))
 
@@ -550,19 +569,20 @@
             src_ref=rows.at[q, h, p, span], dst_ref=rows.at[q, h, p, span], send_sem=send_sem, recv_sem=recv_sem,
             device_id={"samp": to}, device_id_type=MESH)
 
-    def own_copy(q, h, p, to, send_sem, src):
+    def own_copy(q, h, p, to, send_sem, src=None, dst=None):
         return pltpu.make_async_remote_copy(
-            src_ref=rows.at[q, h, p] if src is None else src, dst_ref=rows.at[q, h, p], send_sem=send_sem,
+            src_ref=rows.at[q, h, p] if src is None else src, dst_ref=rows.at[q, h, p] if dst is None else dst,
+            send_sem=send_sem,
             recv_sem=row_recv.at[q // 2, h, p], device_id={"samp": to}, device_id_type=MESH)
 
-    def send_in(q, h, p, src=None, extra=0):
-        own_copy(q, h, p, index(inward, y, core), line_send.at[extra], src).start()
-
-    def send_out(q, h, p, src=None):
-        own_copy(q, h, p, index(outward, y, core), line_send.at[2], src).start()
-
-    def send_side(q, h, p, src=None, extra=0):
-        own_copy(q, h, p, index(z, 1 - y, core), side_send.at[extra], src).start()
+    def send_in(q, h, p, extra=0):
+        own_copy(q, h, p, index(inward, y, core), line_send.at[extra]).start()
+
+    def send_out(q, h, p):
+        own_copy(q, h, p, index(outward, y, core), line_send.at[2]).start()
+
+    def send_side(q, h, p, extra=0):
+        own_copy(q, h, p, index(z, 1 - y, core), side_send.at[extra]).start()
 
     def half_of(q, h, p):
         return jnp.where(jnp.logical_not(is_end) & (q // 4 == depth - 1 - outward), p, h)
@@ -585,25 +605,48 @@
     def part_at(i):
         return lax.rem(part + i, groups)
 
-    def send_own(h, p):
+    def send_own(h, p, skip=0):
         mine = panel.at[h, piece_of(part, p)]
-        send_side(me, h, p, mine)
-        send_in(me, h, p, mine)
+        kept = panel.at[h, pl.ds(pl.multiple_of(part * tile_rows + p * piece_rows + skip, 16), piece_rows - skip)]
+        kept_to = rows.at[me, h, p, pl.ds(skip, piece_rows - skip)]
+        own_copy(me, h, p, index(z, 1 - y, core), side_send.at[0], kept, kept_to).start()
+        own_copy(me, h, p, index(inward, y, core), line_send.at[0], kept, kept_to).start()
 
         @pl.when(jnp.logical_not(is_end))
         def _():
-            send_out(me, h, p, mine)
+            own_copy(me, h, p, index(outward, y, core), line_send.at[2], kept, kept_to).start()
 
         send_core(me, h, p, mine)
         rows[me, h, p] = panel[h, piece_of(part, p), :]
 
+    def scale_raw(slot, q):
+        await_bytes(raw_in.at[slot], raw_sem.at[1 + slot])
+        sent = raw_in[slot]
+        rows[q, part, 0, 0:RAW, :] = jnp.where(sent >= 0.0, (sent - shift) * gain, 0.0).astype(jnp.bfloat16)
+
+    def arrive_near(q, h, p):
+        @pl.when((h == part) & (p == 0))
+        def _():
+            await_bytes(rows.at[q, h, p, pl.ds(RAW, piece_rows - RAW)], row_recv.at[q // 2, h, p])
+
+        @pl.when((h != part) | (p != 0))
+        def _():
+            arrive(q, h, p)
+
     for p in range(PIECES):
         scale_piece(part, p)
-        send_own(part, p)
+        send_own(part, p, 0 if p else RAW)
         scale_piece(other, p)
         panel_copy(other, p).start()
     for p in range(PIECES):
         panel_copy(part, p).start()
+    scale_raw(0, index(z, 1 - y, core))
+    scale_raw(1, index(inward, y, core))
+
+    @pl.when(jnp.logical_not(is_end))
+    def _():
+        scale_raw(2, index(outward, y, core))
+
     for p in range(PIECES):
         await_bytes(panel.at[other, piece_of(part, p)], across_recv.at[p])
         send_own(other, p)
@@ -640,10 +683,10 @@
         def first(t, carry):
             h, p = part_at(t // PIECES), lax.rem(t, PIECES)
             near, beside = index(inward, y, core), index(z, 1 - y, core)
-            arrive(near, h, p)
+            arrive_near(near, h, p)
             send_side(near, h, p)
             send_core(near, h, p)
-            arrive(beside, h, p)
+            arrive_near(beside, h, p)
             send_in(beside, h, p)
             send_core(beside, h, p)
             return carry
@@ -716,9 +759,10 @@
         await_bytes(codes, code_sem.at[1])
         await_bytes(steps, code_sem.at[3])
         arrive_core(index(far_mid, 1 - y, 1 - core), other)
-        await_bytes(rows.at[pl.ds(0, 2)], line_send.at[0])
-        await_bytes(rows.at[pl.ds(0, 2)], side_send.at[0])
-        await_bytes(geno_ref.at[pl.ds(0, (count * piece_rows - (piece_rows - cut)) // 2)], side_send.at[1])
+        await_rows(2 * row_count - RAW, line_send.at[0])
+        await_rows(2 * row_count - RAW, side_send.at[0])
+        await_rows(count * piece_rows - (piece_rows - cut), side_send.at[1])
+        await_bytes(raw_in.at[pl.ds(0, 2)], raw_sem.at[0])
         await_bytes(rows.at[pl.ds(0, 6)], core_send.at[0])
 
     @pl.when(jnp.logical_not(is_end))
@@ -728,7 +772,7 @@
         def first(t, carry):
             h, p = part_at(t // PIECES), lax.rem(t, PIECES)
             end, near, beside = index(outward, y, core), index(inward, y, core), index(z, 1 - y, core)
-            arrive(end, h, p)
+            arrive_near(end, h, p)
 
             @pl.when(p == 0)
             def _():
@@ -740,10 +784,10 @@
 
             send_core(end, h, p)
             column_copy(end, h, p).start()
-            arrive(near, h, p)
+            arrive_near(near, h, p)
             send_out(near, h, p)
             send_core(near, h, p)
-            arrive(beside, h, p)
+            arrive_near(beside, h, p)
             send_core(beside, h, p)
             return carry
 
@@ -846,11 +890,12 @@
 
         lax.fori_loop(0, count, third, 0)
         form(inward, 1 - y)
-        await_bytes(rows.at[pl.ds(0, 2)], line_send.at[0])
+        await_rows(2 * row_count - RAW, line_send.at[0])
         await_bytes(rows.at[0, 0], line_send.at[1])
-        await_bytes(rows.at[pl.ds(0, 2)], line_send.at[2])
-        await_bytes(geno_ref.at[pl.ds(0, (piece_rows - cut) // 2)], line_send.at[3])
-        await_bytes(rows.at[pl.ds(0, 2)], side_send.at[0])
+        await_rows(2 * row_count - RAW, line_send.at[2])
+        await_bytes(raw_in, raw_sem.at[0])
+        await_rows(piece_rows - cut, line_send.at[3])
+        await_rows(2 * row_count - RAW, side_send.at[0])
         await_bytes(rows.at[0, 0], side_send.at[1])
         await_bytes(rows.at[pl.ds(0, 8)], core_send.at[0])
         await_bytes(rows.at[0], across_send.at[1])
@@ -882,10 +927,12 @@
         scratch_shapes=[
             pltpu.VMEM((row_count, snp_count), jnp.float32),
             pltpu.VMEM((row_count, snp_count), jnp.int32),
-            pltpu.VMEM((shards, 2, snp_count), jnp.float32),
+            pltpu.VMEM((shards, 2, snp_count), jnp.int16),
             pltpu.VMEM((groups, groups, tile_rows, snp_count), jnp.bfloat16),
             pltpu.VMEM((units, piece_rows, tile_rows), jnp.int16),
             pltpu.VMEM((units, 1, tile_rows), jnp.float32),
+            pltpu.VMEM((RAW, snp_count), jnp.float32),
+            pltpu.VMEM((3, RAW, snp_count), jnp.float32),
             pltpu.SemaphoreType.DMA((2, LOADS)),
             pltpu.SemaphoreType.DMA((2,)),
             pltpu.SemaphoreType.DMA((2,)),
@@ -896,6 +943,7 @@
             pltpu.SemaphoreType.DMA((shards // 2, groups, PIECES)),
             pltpu.SemaphoreType.DMA((shards // 2, 2)),
             pltpu.SemaphoreType.DMA((6,)),
+            pltpu.SemaphoreType.DMA((4,)),
         ],
         compiler_params=pltpu.CompilerParams(
             collective_id=0, has_side_effects=True, vmem_limit_bytes=VMEM_ALL - FOLDED_SPARE - kept),

time: 84.9 us -> 83.2 us (0.980)
  Pallas kernels: 84.8 us -> 83.1 us
    pallas_call x1, Pallas kernels: 81.5 us -> 79.8 us  [folded_body(): pl.pallas_call(functools.partial(folded, shards, groups), out_shape=outs,...]
where the time goes in v4:
time: 83.2 us; the launch traced here: 83.1 us
  Pallas kernels  83.1 us (100%)
    pallas_call x1, Pallas kernels, folded_body(): pl.pallas_call(functools.partial(folded, shards, groups), out_shape=outs,...  79.8 us
    pallas_call x1, Pallas kernels, folded_body(): pl.pallas_call(functools.partial(folded_finish, shards, groups), out_shap...  3.32 us

profile of v4, /device:TPU:0, one launch (start us, length us, event | category | flops | bytes accessed | tf_op | source)
XLA Modules:
  0.0 83.1 jit_solution(16747445210470383277)
XLA Ops:
  0.0 79.8 %shard_map.28 = (bf16[2,512,1024]{2,1,0:T(8,128)(2,1)S(1)}, bf16[16,2,2,128,1024]{4,3,2,1,0:T(8,128)(2,1)S(1)}, f32[16,256,512]{2,1,0:T(8,128)S(1)}, s16[16,128,256]{2,1,0:T(8,128)(2,1)S(1)}, f32[16,1,256]{2,1,0:T(1,128)S(1)}) custom-call(f32[512,1024]{1,0:T(8,128)} %geno_hbm.1, s32[512,1024]{1,0:T(8,128)} %obs_hbm.1), custom_call_target="tpu_custom_call" | custom-call | tf_op jit(solution)/shard_map/pallas_call | solution.py:922
  79.8 3.3 %shard_map.29 = f32[16,1,256,512]{3,2,1,0:T(8,128)} custom-call(bf16[16,2,2,128,1024]{4,3,2,1,0:T(8,128)(2,1)S(1)} %get-tuple-element.10.rows, bf16[2,512,1024]{2,1,0:T(8,128)(2,1)S(1)} %get-tuple-element.11.panel, f32[16,256,512]{2,1,0:T(8,128)S(1)} %get-tuple-element.12.tiles, s16[16,128,256]{2,1,0:T(8,128)(2,1)S(1)} %get-tuple-element.13.codes, ...), custom_call_target="tpu_custom_call" | custom-call | tf_op jit(solution)/shard_map/pallas_call | solution.py:952

commit v5 on v4

--- a/solution.py
+++ b/solution.py
@@ -446,7 +446,7 @@
     pltpu.make_async_copy(tiles, out_ref.at[:, 0], out_sem.at[0]).wait()
 
 
-def folded(shards, groups, geno_hbm, obs_hbm, panel, rows, tiles, codes, steps, geno_ref, obs_ref, counts, columns,
+def folded(shards, groups, geno_hbm, obs_hbm, panel, rows, tiles, codes, steps, geno_ref, obs_ref, alts, calls, columns,
            made, made_steps, raw, raw_in, load_sem, count_sem, across_send, across_recv, line_send, side_send, core_send, row_recv,
            core_recv, code_sem, raw_sem):
     row_count, snp_count = geno_ref.shape
@@ -491,9 +491,10 @@
         for copy in load(i):
             copy.wait()
         alt, call = lax.fori_loop(i * strips, (i + 1) * strips, add_strip, (alt, call))
-    alt_step = 2.0 * row_count / CODE_TOP
-    both = jnp.concatenate([jnp.sum(alt, axis=0, keepdims=True) * (1.0 / alt_step), jnp.sum(call, axis=0, keepdims=True)])
-    counts[me] = jnp.round(both).astype(jnp.int32).astype(jnp.int16)
+    alts[me] = jnp.sum(alt, axis=0, keepdims=True)
+    call = jnp.sum(call, axis=0, keepdims=True).astype(jnp.int32)
+    half = snp_count // 2
+    calls[me] = jnp.concatenate([call[:, :half], call[:, half:]]).astype(jnp.int16)
 
     pl.semaphore_wait(barrier, shards)
 
@@ -502,9 +503,10 @@
 
         @pl.when(to != me)
         def _():
-            pltpu.make_async_remote_copy(
-                src_ref=counts.at[me], dst_ref=counts.at[me], send_sem=count_sem.at[0], recv_sem=count_sem.at[1],
-                device_id={"samp": to}, device_id_type=MESH).start()
+            for n, sent in enumerate((alts, calls)):
+                pltpu.make_async_remote_copy(
+                    src_ref=sent.at[me], dst_ref=sent.at[me], send_sem=count_sem.at[2 * n],
+                    recv_sem=count_sem.at[2 * n + 1], device_id={"samp": to}, device_id_type=MESH).start()
 
     def await_bytes(ref, sem):
         pltpu.make_async_copy(ref, ref, sem).wait()
@@ -526,12 +528,16 @@
     def _():
         raw_copy(index(outward, y, core), 1).start()
 
-    others = counts.at[pl.ds(0, shards - 1)]
-    await_bytes(others, count_sem.at[1])
-    sums = counts[0].astype(jnp.float32)
+    def await_counts(way):
+        for n, sent in enumerate((alts, calls)):
+            await_bytes(sent.at[pl.ds(0, shards - 1)], count_sem.at[2 * n + way])
+
+    await_counts(1)
+    alt, call = alts[0], calls[0].astype(jnp.int32)
     for s in range(1, shards):
-        sums = sums + counts[s].astype(jnp.float32)
-    frequency = sums[0:1] * alt_step / (2.0 * jnp.maximum(sums[1:2], 1.0))
+        alt, call = alt + alts[s], call + calls[s].astype(jnp.int32)
+    call = jnp.concatenate([call[0:1], call[1:2]], axis=1).astype(jnp.float32)
+    frequency = alt / (2.0 * jnp.maximum(call, 1.0))
     shift = 2.0 * frequency
     gain = lax.rsqrt(jnp.maximum(shift * (1.0 - frequency), var_floor))
 
@@ -902,7 +908,7 @@
         await_bytes(made, code_sem.at[0])
         await_bytes(made_steps, code_sem.at[2])
 
-    await_bytes(others, count_sem.at[0])
+    await_counts(0)
     await_bytes(rows.at[0], across_send.at[0])
 
 
@@ -927,14 +933,15 @@
         scratch_shapes=[
             pltpu.VMEM((row_count, snp_count), jnp.float32),
             pltpu.VMEM((row_count, snp_count), jnp.int32),
-            pltpu.VMEM((shards, 2, snp_count), jnp.int16),
+            pltpu.VMEM((shards, 1, snp_count), jnp.float32),
+            pltpu.VMEM((shards, 2, snp_count // 2), jnp.int16),
             pltpu.VMEM((groups, groups, tile_rows, snp_count), jnp.bfloat16),
             pltpu.VMEM((units, piece_rows, tile_rows), jnp.int16),
             pltpu.VMEM((units, 1, tile_rows), jnp.float32),
             pltpu.VMEM((RAW, snp_count), jnp.float32),
             pltpu.VMEM((3, RAW, snp_count), jnp.float32),
             pltpu.SemaphoreType.DMA((2, LOADS)),
-            pltpu.SemaphoreType.DMA((2,)),
+            pltpu.SemaphoreType.DMA((4,)),
             pltpu.SemaphoreType.DMA((2,)),
             pltpu.SemaphoreType.DMA((PIECES + 2,)),
             pltpu.SemaphoreType.DMA((4,)),

time: 83.2 us -> 83.5 us (level)
  no operation moved by 1% of the time
where the time goes in v5:
time: 83.5 us; the launch traced here: 83.4 us
  Pallas kernels  83.3 us (100%)
    pallas_call x1, Pallas kernels, folded_body(): pl.pallas_call(functools.partial(folded, shards, groups), out_shape=outs,...  80 us
    pallas_call x1, Pallas kernels, folded_body(): pl.pallas_call(functools.partial(folded_finish, shards, groups), out_shap...  3.32 us

profile of v5, /device:TPU:0, one launch (start us, length us, event | category | flops | bytes accessed | tf_op | source)
XLA Modules:
  0.0 83.4 jit_solution(1322001442933385330)
XLA Ops:
  0.0 80.0 %shard_map.28 = (bf16[2,512,1024]{2,1,0:T(8,128)(2,1)S(1)}, bf16[16,2,2,128,1024]{4,3,2,1,0:T(8,128)(2,1)S(1)}, f32[16,256,512]{2,1,0:T(8,128)S(1)}, s16[16,128,256]{2,1,0:T(8,128)(2,1)S(1)}, f32[16,1,256]{2,1,0:T(1,128)S(1)}) custom-call(f32[512,1024]{1,0:T(8,128)} %geno_hbm.1, s32[512,1024]{1,0:T(8,128)} %obs_hbm.1), custom_call_target="tpu_custom_call" | custom-call | tf_op jit(solution)/shard_map/pallas_call | solution.py:928
  80.0 3.3 %shard_map.29 = f32[16,1,256,512]{3,2,1,0:T(8,128)} custom-call(bf16[16,2,2,128,1024]{4,3,2,1,0:T(8,128)(2,1)S(1)} %get-tuple-element.10.rows, bf16[2,512,1024]{2,1,0:T(8,128)(2,1)S(1)} %get-tuple-element.11.panel, f32[16,256,512]{2,1,0:T(8,128)S(1)} %get-tuple-element.12.tiles, s16[16,128,256]{2,1,0:T(8,128)(2,1)S(1)} %get-tuple-element.13.codes, ...), custom_call_target="tpu_custom_call" | custom-call | tf_op jit(solution)/shard_map/pallas_call | solution.py:959

commit v6 on v5

--- a/solution.py
+++ b/solution.py
@@ -706,17 +706,14 @@
             arrive(far, h, p)
             to = index(z, 1 - y, core)
 
-            @pl.when(p == 0)
+            @pl.when(t < count - 1)
             def _():
                 send_side(far, h, p, extra=1)
 
-            @pl.when(p == 1)
+            @pl.when(t == count - 1)
             def _():
                 span_copy(far, h, p, head, to, side_send.at[1], row_recv.at[far // 2, h, p]).start()
-
-            @pl.when((p == 1) & (h == other))
-            def _():
-                span_copy(far, h, p, rest, to, side_send.at[1], code_sem.at[5]).start()
+                span_copy(far, h, p, rest, to, side_send.at[1], code_sem.at[4]).start()
 
             send_core(far, h, p)
             arrive(cross, h, p)
@@ -734,29 +731,21 @@
             h, p = part_at(t // PIECES), lax.rem(t, PIECES)
             q = index(far_mid, 1 - y, core)
 
-            @pl.when(p == 0)
+            @pl.when(t < count - 1)
             def _():
                 arrive(q, h, p)
                 send_core(q, h, p)
 
-            @pl.when(p == 1)
+            @pl.when(t == count - 1)
             def _():
                 await_bytes(rows.at[q, h, p, head], row_recv.at[q // 2, h, p])
                 send_core_span(q, h, p, head)
+                await_bytes(rows.at[q, h, p, rest], code_sem.at[4])
+                send_core_span(q, h, p, rest)
 
             @pl.when(t < 2)
             def _():
                 form(pick(t, (far_mid, inward)), pick(t, (y, 1 - y)))
-
-            @pl.when(t == 2)
-            def _():
-                await_bytes(rows.at[q, part, 1, rest], code_sem.at[4])
-                send_core_span(q, part, 1, rest)
-
-            @pl.when(t == 3)
-            def _():
-                await_bytes(rows.at[q, other, 1, rest], code_sem.at[5])
-                send_core_span(q, other, 1, rest)
 
             return carry
 
@@ -767,7 +756,7 @@
         arrive_core(index(far_mid, 1 - y, 1 - core), other)
         await_rows(2 * row_count - RAW, line_send.at[0])
         await_rows(2 * row_count - RAW, side_send.at[0])
-        await_rows(count * piece_rows - (piece_rows - cut), side_send.at[1])
+        await_rows(count * piece_rows, side_send.at[1])
         await_bytes(raw_in.at[pl.ds(0, 2)], raw_sem.at[0])
         await_bytes(rows.at[pl.ds(0, 6)], core_send.at[0])
 
@@ -803,6 +792,11 @@
         for h in range(groups):
             columns[part, h] = rows[index(outward, y, core), h].reshape(tile_rows, snp_count)
         await_panel()
+
+        def code_copy(source, target, n):
+            return pltpu.make_async_remote_copy(
+                src_ref=source, dst_ref=target, send_sem=code_sem.at[n], recv_sem=code_sem.at[n + 1],
+                device_id={"samp": index(outward, y, core)}, device_id_type=MESH)
 
         def make(side, p, k):
             def per_core(t, carry):
@@ -818,11 +812,7 @@
                 unit = ((side * 2 + which) * PIECES + p) * groups + k
                 made[unit] = jnp.round(term * (CODE_TOP / jnp.maximum(top, TINY))).astype(jnp.int32).astype(jnp.int16)
                 made_steps[unit] = top * (1.0 / CODE_TOP)
-                for n, (source, target) in enumerate(((made, codes), (made_steps, steps))):
-                    pltpu.make_async_remote_copy(
-                        src_ref=source.at[unit], dst_ref=target.at[unit], send_sem=code_sem.at[2 * n],
-                        recv_sem=code_sem.at[2 * n + 1], device_id={"samp": index(outward, y, core)},
-                        device_id_type=MESH).start()
+                code_copy(made.at[unit], codes.at[unit], 0).start()
                 return carry
 
             lax.fori_loop(0, 2, per_core, 0)
@@ -884,9 +874,9 @@
 
             @pl.when(t == 1)
             def _():
-                span_copy(cross, h, p, rest, index(outward, y, core), line_send.at[3], code_sem.at[4]).start()
                 far_core(1, 1)
                 make_list([(1, 1, 0), (1, 1, 1)])
+                code_copy(made_steps, steps, 2).start()
 
             @pl.when(t < 2)
             def _():
@@ -900,7 +890,6 @@
         await_bytes(rows.at[0, 0], line_send.at[1])
         await_rows(2 * row_count - RAW, line_send.at[2])
         await_bytes(raw_in, raw_sem.at[0])
-        await_rows(piece_rows - cut, line_send.at[3])
         await_rows(2 * row_count - RAW, side_send.at[0])
         await_bytes(rows.at[0, 0], side_send.at[1])
         await_bytes(rows.at[pl.ds(0, 8)], core_send.at[0])
@@ -944,12 +933,12 @@
             pltpu.SemaphoreType.DMA((4,)),
             pltpu.SemaphoreType.DMA((2,)),
             pltpu.SemaphoreType.DMA((PIECES + 2,)),
-            pltpu.SemaphoreType.DMA((4,)),
+            pltpu.SemaphoreType.DMA((3,)),
             pltpu.SemaphoreType.DMA((2,)),
             pltpu.SemaphoreType.DMA((1,)),
             pltpu.SemaphoreType.DMA((shards // 2, groups, PIECES)),
             pltpu.SemaphoreType.DMA((shards // 2, 2)),
-            pltpu.SemaphoreType.DMA((6,)),
+            pltpu.SemaphoreType.DMA((5,)),
             pltpu.SemaphoreType.DMA((4,)),
         ],
         compiler_params=pltpu.CompilerParams(

time: 83.5 us -> 83.1 us (level)
  no operation moved by 1% of the time
where the time goes in v6:
time: 83.1 us; the launch traced here: 82.9 us
  Pallas kernels  82.9 us (100%)
    pallas_call x1, Pallas kernels, folded_body(): pl.pallas_call(functools.partial(folded, shards, groups), out_shape=outs,...  79.6 us
    pallas_call x1, Pallas kernels, folded_body(): pl.pallas_call(functools.partial(folded_finish, shards, groups), out_shap...  3.32 us

profile of v6, /device:TPU:0, one launch (start us, length us, event | category | flops | bytes accessed | tf_op | source)
XLA Modules:
  0.0 82.9 jit_solution(3731065283405347634)
XLA Ops:
  0.0 79.6 %shard_map.28 = (bf16[2,512,1024]{2,1,0:T(8,128)(2,1)S(1)}, bf16[16,2,2,128,1024]{4,3,2,1,0:T(8,128)(2,1)S(1)}, f32[16,256,512]{2,1,0:T(8,128)S(1)}, s16[16,128,256]{2,1,0:T(8,128)(2,1)S(1)}, f32[16,1,256]{2,1,0:T(1,128)S(1)}) custom-call(f32[512,1024]{1,0:T(8,128)} %geno_hbm.1, s32[512,1024]{1,0:T(8,128)} %obs_hbm.1), custom_call_target="tpu_custom_call" | custom-call | tf_op jit(solution)/shard_map/pallas_call | solution.py:917
  79.6 3.3 %shard_map.29 = f32[16,1,256,512]{3,2,1,0:T(8,128)} custom-call(bf16[16,2,2,128,1024]{4,3,2,1,0:T(8,128)(2,1)S(1)} %get-tuple-element.10.rows, bf16[2,512,1024]{2,1,0:T(8,128)(2,1)S(1)} %get-tuple-element.11.panel, f32[16,256,512]{2,1,0:T(8,128)S(1)} %get-tuple-element.12.tiles, s16[16,128,256]{2,1,0:T(8,128)(2,1)S(1)} %get-tuple-element.13.codes, ...), custom_call_target="tpu_custom_call" | custom-call | tf_op jit(solution)/shard_map/pallas_call | solution.py:948

commit v7 on v6

--- a/solution.py
+++ b/solution.py
@@ -462,8 +462,8 @@
 
     def load(i):
         block = pl.ds(pl.multiple_of(i * load_rows, load_rows), load_rows)
-        return (pltpu.make_async_copy(geno_hbm.at[block], geno_ref.at[block], load_sem.at[0, i]),
-                pltpu.make_async_copy(obs_hbm.at[block], obs_ref.at[block], load_sem.at[1, i]))
+        return (pltpu.make_async_copy(geno_hbm.at[block], geno_ref.at[block], load_sem.at[i]),
+                pltpu.make_async_copy(obs_hbm.at[block], obs_ref.at[block], load_sem.at[i]))
 
     for i in range(LOADS):
         for copy in load(i):
@@ -488,8 +488,8 @@
     alt, call = zero, zero
     strips = load_rows // STRIP
     for i in range(LOADS):
-        for copy in load(i):
-            copy.wait()
+        loaded = geno_ref.at[pl.ds(0, 2 * load_rows)]
+        pltpu.make_async_copy(loaded, loaded, load_sem.at[i]).wait()
         alt, call = lax.fori_loop(i * strips, (i + 1) * strips, add_strip, (alt, call))
     alts[me] = jnp.sum(alt, axis=0, keepdims=True)
     call = jnp.sum(call, axis=0, keepdims=True).astype(jnp.int32)
@@ -575,11 +575,14 @@
             src_ref=rows.at[q, h, p, span], dst_ref=rows.at[q, h, p, span], send_sem=send_sem, recv_sem=recv_sem,
             device_id={"samp": to}, device_id_type=MESH)
 
+    def slot_of(q, at):
+        return lax.rem(q // 2 - at // 2 + shards // 2, shards // 2) - 1
+
     def own_copy(q, h, p, to, send_sem, src=None, dst=None):
         return pltpu.make_async_remote_copy(
             src_ref=rows.at[q, h, p] if src is None else src, dst_ref=rows.at[q, h, p] if dst is None else dst,
             send_sem=send_sem,
-            recv_sem=row_recv.at[q // 2, h, p], device_id={"samp": to}, device_id_type=MESH)
+            recv_sem=row_recv.at[slot_of(q, to), h, p], device_id={"samp": to}, device_id_type=MESH)
 
     def send_in(q, h, p, extra=0):
         own_copy(q, h, p, index(inward, y, core), line_send.at[extra]).start()
@@ -590,23 +593,28 @@
     def send_side(q, h, p, extra=0):
         own_copy(q, h, p, index(z, 1 - y, core), side_send.at[extra]).start()
 
-    def half_of(q, h, p):
-        return jnp.where(jnp.logical_not(is_end) & (q // 4 == depth - 1 - outward), p, h)
+    def core_slot(q, h, p):
+        late = jnp.where(is_end, (q // 2 == (depth - 1 - inward) * 2 + 1 - y) & (h != part),
+                         (q // 4 == depth - 1 - outward) & (p == 1))
+        return jnp.where(late, late_slot(q), q // 2)
+
+    def late_slot(q):
+        return shards // 2 + lax.rem(q // 2, 2)
 
     def send_core(q, h, p, src=None):
         pltpu.make_async_remote_copy(
             src_ref=rows.at[q, h, p] if src is None else src, dst_ref=rows.at[q, h, p], send_sem=core_send.at[0],
-            recv_sem=core_recv.at[q // 2, half_of(q, h, p)], device_id={"samp": index(z, y, 1 - core)},
+            recv_sem=core_recv.at[core_slot(q, h, p)], device_id={"samp": index(z, y, 1 - core)},
             device_id_type=MESH).start()
 
     def send_core_span(q, h, p, span):
-        span_copy(q, h, p, span, index(z, y, 1 - core), core_send.at[0], core_recv.at[q // 2, half_of(q, h, p)]).start()
+        span_copy(q, h, p, span, index(z, y, 1 - core), core_send.at[0], core_recv.at[core_slot(q, h, p)]).start()
 
     def arrive(q, h, p):
-        await_bytes(rows.at[q, h, p], row_recv.at[q // 2, h, p])
-
-    def arrive_core(q, half):
-        await_bytes(rows.at[q, 0], core_recv.at[q // 2, half])
+        await_bytes(rows.at[q, h, p], row_recv.at[slot_of(q, me), h, p])
+
+    def arrive_core(q, late):
+        await_bytes(rows.at[q, 0], core_recv.at[late_slot(q) if late else q // 2])
 
     def part_at(i):
         return lax.rem(part + i, groups)
@@ -633,7 +641,7 @@
     def arrive_near(q, h, p):
         @pl.when((h == part) & (p == 0))
         def _():
-            await_bytes(rows.at[q, h, p, pl.ds(RAW, piece_rows - RAW)], row_recv.at[q // 2, h, p])
+            await_bytes(rows.at[q, h, p, pl.ds(RAW, piece_rows - RAW)], row_recv.at[slot_of(q, me), h, p])
 
         @pl.when((h != part) | (p != 0))
         def _():
@@ -663,8 +671,10 @@
             if wait:
                 @pl.when(t == 1)
                 def _():
-                    for half in (range(2) if parts is None else parts):
-                        arrive_core(q, half)
+                    if parts is None:
+                        await_bytes(rows.at[q], core_recv.at[q // 2])
+                    else:
+                        arrive_core(q, False)
 
             tiles[q] = product(rows, panel, q, range(groups) if parts is None else parts)
             return carry
@@ -712,7 +722,7 @@
 
             @pl.when(t == count - 1)
             def _():
-                span_copy(far, h, p, head, to, side_send.at[1], row_recv.at[far // 2, h, p]).start()
+                span_copy(far, h, p, head, to, side_send.at[1], row_recv.at[slot_of(far, to), h, p]).start()
                 span_copy(far, h, p, rest, to, side_send.at[1], code_sem.at[4]).start()
 
             send_core(far, h, p)
@@ -738,7 +748,7 @@
 
             @pl.when(t == count - 1)
             def _():
-                await_bytes(rows.at[q, h, p, head], row_recv.at[q // 2, h, p])
+                await_bytes(rows.at[q, h, p, head], row_recv.at[slot_of(q, me), h, p])
                 send_core_span(q, h, p, head)
                 await_bytes(rows.at[q, h, p, rest], code_sem.at[4])
                 send_core_span(q, h, p, rest)
@@ -747,13 +757,16 @@
             def _():
                 form(pick(t, (far_mid, inward)), pick(t, (y, 1 - y)))
 
+            @pl.when(t == 2)
+            def _():
+                form(far_mid, 1 - y, [part])
+
             return carry
 
         lax.fori_loop(0, count, third, 0)
-        form(far_mid, 1 - y, [part])
         await_bytes(codes, code_sem.at[1])
         await_bytes(steps, code_sem.at[3])
-        arrive_core(index(far_mid, 1 - y, 1 - core), other)
+        arrive_core(index(far_mid, 1 - y, 1 - core), True)
         await_rows(2 * row_count - RAW, line_send.at[0])
         await_rows(2 * row_count - RAW, side_send.at[0])
         await_rows(count * piece_rows, side_send.at[1])
@@ -818,7 +831,7 @@
             lax.fori_loop(0, 2, per_core, 0)
 
         def far_core(side, p):
-            arrive_core(index(far, jnp.where(side == 0, y, 1 - y), 1 - core), p)
+            arrive_core(index(far, jnp.where(side == 0, y, 1 - y), 1 - core), p == 1)
 
         def make_list(listed):
             def per_entry(i, carry):
@@ -929,15 +942,15 @@
             pltpu.VMEM((units, 1, tile_rows), jnp.float32),
             pltpu.VMEM((RAW, snp_count), jnp.float32),
             pltpu.VMEM((3, RAW, snp_count), jnp.float32),
-            pltpu.SemaphoreType.DMA((2, LOADS)),
+            pltpu.SemaphoreType.DMA((LOADS,)),
             pltpu.SemaphoreType.DMA((4,)),
             pltpu.SemaphoreType.DMA((2,)),
             pltpu.SemaphoreType.DMA((PIECES + 2,)),
             pltpu.SemaphoreType.DMA((3,)),
             pltpu.SemaphoreType.DMA((2,)),
             pltpu.SemaphoreType.DMA((1,)),
-            pltpu.SemaphoreType.DMA((shards // 2, groups, PIECES)),
-            pltpu.SemaphoreType.DMA((shards // 2, 2)),
+            pltpu.SemaphoreType.DMA((shards // 2 - 1, groups, PIECES)),
+            pltpu.SemaphoreType.DMA((shards // 2 + 2,)),
             pltpu.SemaphoreType.DMA((5,)),
             pltpu.SemaphoreType.DMA((4,)),
         ],

time: 83.1 us -> 82.8 us (level)
  no operation moved by 1% of the time
where the time goes in v7:
time: 82.8 us; the launch traced here: 82.7 us
  Pallas kernels  82.7 us (100%)
    pallas_call x1, Pallas kernels, folded_body(): pl.pallas_call(functools.partial(folded, shards, groups), out_shape=outs,...  79.4 us
    pallas_call x1, Pallas kernels, folded_body(): pl.pallas_call(functools.partial(folded_finish, shards, groups), out_shap...  3.32 us

profile of v7, /device:TPU:0, one launch (start us, length us, event | category | flops | bytes accessed | tf_op | source)
XLA Modules:
  0.0 82.7 jit_solution(8687596183880386739)
XLA Ops:
  0.0 79.4 %shard_map.28 = (bf16[2,512,1024]{2,1,0:T(8,128)(2,1)S(1)}, bf16[16,2,2,128,1024]{4,3,2,1,0:T(8,128)(2,1)S(1)}, f32[16,256,512]{2,1,0:T(8,128)S(1)}, s16[16,128,256]{2,1,0:T(8,128)(2,1)S(1)}, f32[16,1,256]{2,1,0:T(1,128)S(1)}) custom-call(f32[512,1024]{1,0:T(8,128)} %geno_hbm.1, s32[512,1024]{1,0:T(8,128)} %obs_hbm.1), custom_call_target="tpu_custom_call" | custom-call | tf_op jit(solution)/shard_map/pallas_call | solution.py:930
  79.4 3.3 %shard_map.29 = f32[16,1,256,512]{3,2,1,0:T(8,128)} custom-call(bf16[16,2,2,128,1024]{4,3,2,1,0:T(8,128)(2,1)S(1)} %get-tuple-element.10.rows, bf16[2,512,1024]{2,1,0:T(8,128)(2,1)S(1)} %get-tuple-element.11.panel, f32[16,256,512]{2,1,0:T(8,128)S(1)} %get-tuple-element.12.tiles, s16[16,128,256]{2,1,0:T(8,128)(2,1)S(1)} %get-tuple-element.13.codes, ...), custom_call_target="tpu_custom_call" | custom-call | tf_op jit(solution)/shard_map/pallas_call | solution.py:961

commit v8 on v7

--- a/solution.py
+++ b/solution.py
@@ -496,6 +496,8 @@
     half = snp_count // 2
     calls[me] = jnp.concatenate([call[:, :half], call[:, half:]]).astype(jnp.int16)
 
+    early = pl.ds(pl.multiple_of(part * tile_rows, tile_rows), RAW)
+    raw[...] = jnp.where(obs_ref[early, :] > 0, geno_ref[early, :], -1.0)
     pl.semaphore_wait(barrier, shards)
 
     for step in range(shards):
@@ -519,8 +521,6 @@
             src_ref=raw, dst_ref=raw_in.at[slot], send_sem=raw_sem.at[0], recv_sem=raw_sem.at[1 + slot],
             device_id={"samp": to}, device_id_type=MESH)
 
-    early = pl.ds(pl.multiple_of(part * tile_rows, tile_rows), RAW)
-    raw[...] = jnp.where(obs_ref[early, :] > 0, geno_ref[early, :], -1.0)
     raw_copy(index(z, 1 - y, core), 0).start()
     raw_copy(index(inward, y, core), jnp.where(is_end, 2, 1)).start()
 

time: 82.8 us -> 82.8 us (level)
  no operation moved by 1% of the time
where the time goes in v8:
time: 82.8 us; the launch traced here: 82.7 us
  Pallas kernels  82.7 us (100%)
    pallas_call x1, Pallas kernels, folded_body(): pl.pallas_call(functools.partial(folded, shards, groups), out_shape=outs,...  79.4 us
    pallas_call x1, Pallas kernels, folded_body(): pl.pallas_call(functools.partial(folded_finish, shards, groups), out_shap...  3.32 us

profile of v8, /device:TPU:0, one launch (start us, length us, event | category | flops | bytes accessed | tf_op | source)
XLA Modules:
  0.0 82.7 jit_solution(8059376037709235688)
XLA Ops:
  0.0 79.4 %shard_map.28 = (bf16[2,512,1024]{2,1,0:T(8,128)(2,1)S(1)}, bf16[16,2,2,128,1024]{4,3,2,1,0:T(8,128)(2,1)S(1)}, f32[16,256,512]{2,1,0:T(8,128)S(1)}, s16[16,128,256]{2,1,0:T(8,128)(2,1)S(1)}, f32[16,1,256]{2,1,0:T(1,128)S(1)}) custom-call(f32[512,1024]{1,0:T(8,128)} %geno_hbm.1, s32[512,1024]{1,0:T(8,128)} %obs_hbm.1), custom_call_target="tpu_custom_call" | custom-call | tf_op jit(solution)/shard_map/pallas_call | solution.py:930
  79.4 3.3 %shard_map.29 = f32[16,1,256,512]{3,2,1,0:T(8,128)} custom-call(bf16[16,2,2,128,1024]{4,3,2,1,0:T(8,128)(2,1)S(1)} %get-tuple-element.10.rows, bf16[2,512,1024]{2,1,0:T(8,128)(2,1)S(1)} %get-tuple-element.11.panel, f32[16,256,512]{2,1,0:T(8,128)S(1)} %get-tuple-element.12.tiles, s16[16,128,256]{2,1,0:T(8,128)(2,1)S(1)} %get-tuple-element.13.codes, ...), custom_call_target="tpu_custom_call" | custom-call | tf_op jit(solution)/shard_map/pallas_call | solution.py:961

commit v9 on v8

--- a/solution.py
+++ b/solution.py
@@ -518,7 +518,7 @@
 
     def raw_copy(to, slot):
         return pltpu.make_async_remote_copy(
-            src_ref=raw, dst_ref=raw_in.at[slot], send_sem=raw_sem.at[0], recv_sem=raw_sem.at[1 + slot],
+            src_ref=raw, dst_ref=raw_in.at[slot], send_sem=raw_sem.at[0], recv_sem=raw_sem.at[1],
             device_id={"samp": to}, device_id_type=MESH)
 
     raw_copy(index(z, 1 - y, core), 0).start()
@@ -634,7 +634,6 @@
         rows[me, h, p] = panel[h, piece_of(part, p), :]
 
     def scale_raw(slot, q):
-        await_bytes(raw_in.at[slot], raw_sem.at[1 + slot])
         sent = raw_in[slot]
         rows[q, part, 0, 0:RAW, :] = jnp.where(sent >= 0.0, (sent - shift) * gain, 0.0).astype(jnp.bfloat16)
 
@@ -654,6 +653,15 @@
         panel_copy(other, p).start()
     for p in range(PIECES):
         panel_copy(part, p).start()
+
+    @pl.when(is_end)
+    def _():
+        await_bytes(raw_in.at[pl.ds(0, 2)], raw_sem.at[1])
+
+    @pl.when(jnp.logical_not(is_end))
+    def _():
+        await_bytes(raw_in, raw_sem.at[1])
+
     scale_raw(0, index(z, 1 - y, core))
     scale_raw(1, index(inward, y, core))
 
@@ -952,7 +960,7 @@
             pltpu.SemaphoreType.DMA((shards // 2 - 1, groups, PIECES)),
             pltpu.SemaphoreType.DMA((shards // 2 + 2,)),
             pltpu.SemaphoreType.DMA((5,)),
-            pltpu.SemaphoreType.DMA((4,)),
+            pltpu.SemaphoreType.DMA((2,)),
         ],
         compiler_params=pltpu.CompilerParams(
             collective_id=0, has_side_effects=True, vmem_limit_bytes=VMEM_ALL - FOLDED_SPARE - kept),

time: 82.8 us -> 82.8 us (level)
  no operation moved by 1% of the time
where the time goes in v9:
time: 82.8 us; the launch traced here: 82.7 us
  Pallas kernels  82.7 us (100%)
    pallas_call x1, Pallas kernels, folded_body(): pl.pallas_call(functools.partial(folded, shards, groups), out_shape=outs,...  79.4 us
    pallas_call x1, Pallas kernels, folded_body(): pl.pallas_call(functools.partial(folded_finish, shards, groups), out_shap...  3.32 us

profile of v9, /device:TPU:0, one launch (start us, length us, event | category | flops | bytes accessed | tf_op | source)
XLA Modules:
  0.0 82.7 jit_solution(1632298669128489804)
XLA Ops:
  0.0 79.4 %shard_map.28 = (bf16[2,512,1024]{2,1,0:T(8,128)(2,1)S(1)}, bf16[16,2,2,128,1024]{4,3,2,1,0:T(8,128)(2,1)S(1)}, f32[16,256,512]{2,1,0:T(8,128)S(1)}, s16[16,128,256]{2,1,0:T(8,128)(2,1)S(1)}, f32[16,1,256]{2,1,0:T(1,128)S(1)}) custom-call(f32[512,1024]{1,0:T(8,128)} %geno_hbm.1, s32[512,1024]{1,0:T(8,128)} %obs_hbm.1), custom_call_target="tpu_custom_call" | custom-call | tf_op jit(solution)/shard_map/pallas_call | solution.py:938
  79.4 3.3 %shard_map.29 = f32[16,1,256,512]{3,2,1,0:T(8,128)} custom-call(bf16[16,2,2,128,1024]{4,3,2,1,0:T(8,128)(2,1)S(1)} %get-tuple-element.10.rows, bf16[2,512,1024]{2,1,0:T(8,128)(2,1)S(1)} %get-tuple-element.11.panel, f32[16,256,512]{2,1,0:T(8,128)S(1)} %get-tuple-element.12.tiles, s16[16,128,256]{2,1,0:T(8,128)(2,1)S(1)} %get-tuple-element.13.codes, ...), custom_call_target="tpu_custom_call" | custom-call | tf_op jit(solution)/shard_map/pallas_call | solution.py:969
